TPU v7x, 32 devices: a whole 2x2x4 slice. The times are simulated.
32 devices in a mesh: dp: 2 (over x), cpo: 4 (over z), cpi: 4 (over y, core).
Axes of the slice: x: 2, y: 2, z: 4, core: 2. Of those that a mesh axis runs over, the one named last changes fastest.
Arguments:
- hidden: bfloat16 [6144, 2560], P(('dp', 'cpo', 'cpi')), parts along dimension 0
- w_q: bfloat16 [2560, 8, 256], replicated
- w_k: bfloat16 [2560, 4, 256], replicated
- w_v: bfloat16 [2560, 4, 256], replicated
- w_o: bfloat16 [8, 256, 2560], replicated
Outputs:
- output: bfloat16 [6144, 2560], P(('dp', 'cpo', 'cpi')), parts along dimension 0
There are 2 independent parts. A program takes and returns all parts, laid end to end along the dimension named above; an argument that names none is the same for every part.
All inputs are finite; a program needn't handle non-finite values.
Results may differ from a plain program's by a relative error of at most 0.00476169.
Values are sent between devices in bfloat16 or wider.
A program may use at most 1 GiB of HBM per device.

v0:
```python
import jax
import jax.numpy as jnp
from jax import lax
from jax.sharding import PartitionSpec as P

WINDOW = 2048
ROPE_BASE = 10000.0


def rope_rotate(vals, positions):
    half_dim = vals.shape[-1] // 2
    inv_freq = ROPE_BASE ** (-jnp.arange(half_dim, dtype=jnp.float32) * 2.0 / vals.shape[-1])
    angles = positions.astype(jnp.float32)[..., None] * inv_freq
    cos_t = jnp.cos(angles)[..., None, :]
    sin_t = jnp.sin(angles)[..., None, :]
    lower_half = vals[..., :half_dim]
    upper_half = vals[..., half_dim:]
    return jnp.concatenate([lower_half * cos_t - upper_half * sin_t, upper_half * cos_t + lower_half * sin_t], axis=-1)


def project_local(hidden, w_q, w_k, w_v, positions):
    q_rot = rope_rotate(jnp.einsum('td,dhe->the', hidden, w_q, preferred_element_type=jnp.float32), positions).astype(jnp.bfloat16)
    k_rot = rope_rotate(jnp.einsum('td,dhe->the', hidden, w_k, preferred_element_type=jnp.float32), positions).astype(jnp.bfloat16)
    v_val = jnp.einsum('td,dhe->the', hidden, w_v, preferred_element_type=jnp.float32).astype(jnp.bfloat16)
    return q_rot, k_rot, v_val


def attend_step(soft_state, q_grp, k_blk, v_blk, back_step, source_ok):
    run_max, run_sum, run_acc = soft_state
    tok_count = q_grp.shape[0]
    score_scale = q_grp.shape[-1] ** -0.5
    scores = jnp.einsum('tkgd,skd->kgts', q_grp, k_blk, preferred_element_type=jnp.float32) * score_scale
    tok_idx = jnp.arange(tok_count)
    pos_gap = back_step * tok_count + tok_idx[:, None] - tok_idx[None, :]
    allowed = (pos_gap >= 0) & (pos_gap < WINDOW) & source_ok
    scores = jnp.where(allowed, scores, -jnp.inf)
    new_max = jnp.maximum(run_max, jnp.max(scores, axis=-1))
    exp_scores = jnp.exp(scores - new_max[..., None])
    rescale = jnp.exp(run_max - new_max)
    run_sum = run_sum * rescale + jnp.sum(exp_scores, axis=-1)
    run_acc = run_acc * rescale[..., None] + jnp.einsum('kgts,skd->kgtd', exp_scores.astype(jnp.bfloat16), v_blk, preferred_element_type=jnp.float32)
    return new_max, run_sum, run_acc


def finish_output(soft_state, w_o):
    run_max, run_sum, run_acc = soft_state
    heads_kv, group_size = run_acc.shape[0], run_acc.shape[1]
    attended = (run_acc / run_sum[..., None]).astype(jnp.bfloat16)
    w_grp = w_o.reshape(heads_kv, group_size, w_o.shape[1], w_o.shape[2])
    return jnp.einsum('kgtd,kgde->te', attended, w_grp, preferred_element_type=jnp.float32).astype(jnp.bfloat16)


def solution(mesh):
    n_outer = mesh.shape['cpo']
    n_inner = mesh.shape['cpi']
    n_shards = n_outer * n_inner
    shift_perm = [(source, source + 1) for source in range(n_shards - 1)]

    def local_fn(hidden, w_q, w_k, w_v, w_o):
        tok_count = hidden.shape[0]
        heads_q, head_dim = w_q.shape[1], w_q.shape[2]
        heads_kv = w_k.shape[1]
        group_size = heads_q // heads_kv
        n_back = min((WINDOW + tok_count - 2) // tok_count, n_shards - 1)
        shard_rank = lax.axis_index('cpo') * n_inner + lax.axis_index('cpi')
        positions = shard_rank * tok_count + jnp.arange(tok_count)
        q_rot, k_cur, v_cur = project_local(hidden, w_q, w_k, w_v, positions)
        q_grp = q_rot.reshape(tok_count, heads_kv, group_size, head_dim)
        soft_state = (jnp.full((heads_kv, group_size, tok_count), -jnp.inf, jnp.float32),
                      jnp.zeros((heads_kv, group_size, tok_count), jnp.float32),
                      jnp.zeros((heads_kv, group_size, tok_count, head_dim), jnp.float32))
        soft_state = attend_step(soft_state, q_grp, k_cur, v_cur, 0, True)
        for back_step in range(1, n_back + 1):
            k_cur = lax.ppermute(k_cur, ('cpo', 'cpi'), shift_perm)
            v_cur = lax.ppermute(v_cur, ('cpo', 'cpi'), shift_perm)
            soft_state = attend_step(soft_state, q_grp, k_cur, v_cur, back_step, shard_rank >= back_step)
        return finish_output(soft_state, w_o)

    return jax.shard_map(local_fn, mesh=mesh,
                         in_specs=(P(('dp', 'cpo', 'cpi'), None), P(), P(), P(), P()),
                         out_specs=P(('dp', 'cpo', 'cpi'), None), check_vma=False)
```

profile of v0, /device:TPU:26, one launch (start us, length us, event | category | flops | bytes accessed | tf_op | source)
XLA Modules:
  0.0 157.9 jit_solution(7442073683231763655)
XLA Ops:
  1.2 4.2 %fusion.6 = f32[192,4,256]{2,0,1:T(8,128)S(1)} fusion(bf16[2560,4,256]{2,1,0:T(4,128)(2,1)} %param.7, bf16[192,2560]{1,0:T(8,128)(2,1)S(1)} %copy-done), kind=kOutput, calls=%fused_computation.6 | convolution fusion | flops 1006632960 | bytes 7012352 | tf_op jit(solution)/shard_map/td,dhe->the/dot_general | solution.py:23
  6.3 2.0 %collective-permute-start = (bf16[192,4,256]{2,0,1:T(8,128)(2,1)}, bf16[192,4,256]{2,0,1:T(8,128)(2,1)}, u32[]{:S(2)}, u32[]{:S(2)}) collective-permute-start(bf16[192,4,256]{2,0,1:T(8,128)(2,1)} %pad_maximum_fusion.1), channel_id=1, source_target_pairs={{0,1},{1,2},{2,3},{3,4},{4,5},{5,6},{6,7},{7,8},{8,9},{9,10},{10,1... | collective-permute-start | bytes 1179656 | tf_op jit(solution)/shard_map/ppermute | solution.py:74
  8.4 1.9 %fusion.38 = bf16[192,4,256]{2,0,1:T(8,128)(2,1)} fusion(bf16[2560,4,256]{2,1,0:T(4,128)(2,1)S(1)} %copy-done.9, bf16[192,2560]{1,0:T(8,128)(2,1)S(1)} %copy-done), kind=kOutput, calls=%fused_computation.59 | convolution fusion | flops 1006829568 | bytes 6619136 | tf_op jit(solution)/shard_map/td,dhe->the/dot_general | solution.py:24
  10.3 3.5 %collective-permute-start.1 = (bf16[192,4,256]{2,0,1:T(8,128)(2,1)}, bf16[192,4,256]{2,0,1:T(8,128)(2,1)}, u32[]{:S(2)}, u32[]{:S(2)}) collective-permute-start(bf16[192,4,256]{2,0,1:T(8,128)(2,1)} %fusion.38), channel_id=1, source_target_pairs={{0,1},{1,2},{2,3},{3,4},{4,5},{5,6},{6,7},{7,8},{8,9},{9,10},{10,1... | collective-permute-start | bytes 1179656 | tf_op jit(solution)/shard_map/ppermute | solution.py:75
  13.9 2.2 %fusion.2 = f32[192,8,256]{2,0,1:T(8,128)S(1)} fusion(bf16[2560,8,256]{2,1,0:T(8,128)(2,1)S(1)} %bitcast.186, bf16[192,2560]{1,0:T(8,128)(2,1)S(1)} %copy-done), kind=kOutput, calls=%fused_computation.2 | convolution fusion | flops 2013265920 | bytes 13041664 | tf_op jit(solution)/shard_map/td,dhe->the/dot_general | solution.py:22
  17.8 1.9 %collective-permute-start.2 = (bf16[192,4,256]{2,0,1:T(8,128)(2,1)}, bf16[192,4,256]{2,0,1:T(8,128)(2,1)}, u32[]{:S(2)}, u32[]{:S(2)}) collective-permute-start(bf16[192,4,256]{2,0,1:T(8,128)(2,1)} %collective-permute-done), channel_id=1, source_target_pairs={{0,1},{1,2},{2,3},{3,4},{4,5},{5,6},{6,7},{7,8},{8,9},{9,10},{10,1... | collective-permute-start | bytes 1179656 | tf_op jit(solution)/shard_map/ppermute | solution.py:74
  20.6 1.9 %collective-permute-start.3 = (bf16[192,4,256]{2,0,1:T(8,128)(2,1)}, bf16[192,4,256]{2,0,1:T(8,128)(2,1)}, u32[]{:S(2)}, u32[]{:S(2)}) collective-permute-start(bf16[192,4,256]{2,0,1:T(8,128)(2,1)} %collective-permute-done.1), channel_id=1, source_target_pairs={{0,1},{1,2},{2,3},{3,4},{4,5},{5,6},{6,7},{7,8},{8,9},{9,10},{10,1... | collective-permute-start | bytes 1179656 | tf_op jit(solution)/shard_map/ppermute | solution.py:75
  23.2 4.6 %collective-permute-done.2 = bf16[192,4,256]{2,0,1:T(8,128)(2,1)} collective-permute-done((bf16[192,4,256]{2,0,1:T(8,128)(2,1)}, bf16[192,4,256]{2,0,1:T(8,128)(2,1)}, u32[]{:S(2)}, u32[]{:S(2)}) %collective-permute-start.2) | collective-permute-done | bytes 393248 | tf_op jit(solution)/shard_map/ppermute | solution.py:74
  27.8 1.9 %collective-permute-start.4 = (bf16[192,4,256]{2,0,1:T(8,128)(2,1)}, bf16[192,4,256]{2,0,1:T(8,128)(2,1)}, u32[]{:S(2)}, u32[]{:S(2)}) collective-permute-start(bf16[192,4,256]{2,0,1:T(8,128)(2,1)} %collective-permute-done.2), channel_id=1, source_target_pairs={{0,1},{1,2},{2,3},{3,4},{4,5},{5,6},{6,7},{7,8},{8,9},{9,10},{10,1... | collective-permute-start | bytes 1179656 | tf_op jit(solution)/shard_map/ppermute | solution.py:74
  30.1 2.0 %collective-permute-done.3 = bf16[192,4,256]{2,0,1:T(8,128)(2,1)} collective-permute-done((bf16[192,4,256]{2,0,1:T(8,128)(2,1)}, bf16[192,4,256]{2,0,1:T(8,128)(2,1)}, u32[]{:S(2)}, u32[]{:S(2)}) %collective-permute-start.3) | collective-permute-done | bytes 393248 | tf_op jit(solution)/shard_map/ppermute | solution.py:75
  32.0 1.9 %collective-permute-start.5 = (bf16[192,4,256]{2,0,1:T(8,128)(2,1)}, bf16[192,4,256]{2,0,1:T(8,128)(2,1)}, u32[]{:S(2)}, u32[]{:S(2)}) collective-permute-start(bf16[192,4,256]{2,0,1:T(8,128)(2,1)} %collective-permute-done.3), channel_id=1, source_target_pairs={{0,1},{1,2},{2,3},{3,4},{4,5},{5,6},{6,7},{7,8},{8,9},{9,10},{10,1... | collective-permute-start | bytes 1179656 | tf_op jit(solution)/shard_map/ppermute | solution.py:75
  34.0 3.8 %collective-permute-done.4 = bf16[192,4,256]{2,0,1:T(8,128)(2,1)} collective-permute-done((bf16[192,4,256]{2,0,1:T(8,128)(2,1)}, bf16[192,4,256]{2,0,1:T(8,128)(2,1)}, u32[]{:S(2)}, u32[]{:S(2)}) %collective-permute-start.4) | collective-permute-done | bytes 393248 | tf_op jit(solution)/shard_map/ppermute | solution.py:74
  37.8 1.9 %collective-permute-start.6 = (bf16[192,4,256]{2,0,1:T(8,128)(2,1)}, bf16[192,4,256]{2,0,1:T(8,128)(2,1)}, u32[]{:S(2)}, u32[]{:S(2)}) collective-permute-start(bf16[192,4,256]{2,0,1:T(8,128)(2,1)} %collective-permute-done.4), channel_id=1, source_target_pairs={{0,1},{1,2},{2,3},{3,4},{4,5},{5,6},{6,7},{7,8},{8,9},{9,10},{10,1... | collective-permute-start | bytes 1179656 | tf_op jit(solution)/shard_map/ppermute | solution.py:74
  39.8 2.2 %collective-permute-done.5 = bf16[192,4,256]{2,0,1:T(8,128)(2,1)} collective-permute-done((bf16[192,4,256]{2,0,1:T(8,128)(2,1)}, bf16[192,4,256]{2,0,1:T(8,128)(2,1)}, u32[]{:S(2)}, u32[]{:S(2)}) %collective-permute-start.5) | collective-permute-done | bytes 393248 | tf_op jit(solution)/shard_map/ppermute | solution.py:75
  42.0 1.9 %collective-permute-start.7 = (bf16[192,4,256]{2,0,1:T(8,128)(2,1)}, bf16[192,4,256]{2,0,1:T(8,128)(2,1)}, u32[]{:S(2)}, u32[]{:S(2)}) collective-permute-start(bf16[192,4,256]{2,0,1:T(8,128)(2,1)} %collective-permute-done.5), channel_id=1, source_target_pairs={{0,1},{1,2},{2,3},{3,4},{4,5},{5,6},{6,7},{7,8},{8,9},{9,10},{10,1... | collective-permute-start | bytes 1179656 | tf_op jit(solution)/shard_map/ppermute | solution.py:75
  44.0 3.8 %collective-permute-done.6 = bf16[192,4,256]{2,0,1:T(8,128)(2,1)} collective-permute-done((bf16[192,4,256]{2,0,1:T(8,128)(2,1)}, bf16[192,4,256]{2,0,1:T(8,128)(2,1)}, u32[]{:S(2)}, u32[]{:S(2)}) %collective-permute-start.6) | collective-permute-done | bytes 393248 | tf_op jit(solution)/shard_map/ppermute | solution.py:74
  47.8 1.9 %collective-permute-start.8 = (bf16[192,4,256]{2,0,1:T(8,128)(2,1)}, bf16[192,4,256]{2,0,1:T(8,128)(2,1)}, u32[]{:S(2)}, u32[]{:S(2)}) collective-permute-start(bf16[192,4,256]{2,0,1:T(8,128)(2,1)} %collective-permute-done.6), channel_id=1, source_target_pairs={{0,1},{1,2},{2,3},{3,4},{4,5},{5,6},{6,7},{7,8},{8,9},{9,10},{10,1... | collective-permute-start | bytes 1179656 | tf_op jit(solution)/shard_map/ppermute | solution.py:74
  54.0 3.8 %collective-permute-done.8 = bf16[192,4,256]{2,0,1:T(8,128)(2,1)} collective-permute-done((bf16[192,4,256]{2,0,1:T(8,128)(2,1)}, bf16[192,4,256]{2,0,1:T(8,128)(2,1)}, u32[]{:S(2)}, u32[]{:S(2)}) %collective-permute-start.8) | collective-permute-done | bytes 393248 | tf_op jit(solution)/shard_map/ppermute | solution.py:74
  57.8 1.9 %collective-permute-start.10 = (bf16[192,4,256]{2,0,1:T(8,128)(2,1)}, bf16[192,4,256]{2,0,1:T(8,128)(2,1)}, u32[]{:S(2)}, u32[]{:S(2)}) collective-permute-start(bf16[192,4,256]{2,0,1:T(8,128)(2,1)} %collective-permute-done.8), channel_id=1, source_target_pairs={{0,1},{1,2},{2,3},{3,4},{4,5},{5,6},{6,7},{7,8},{8,9},{9,10},{10,1... | collective-permute-start | bytes 1179656 | tf_op jit(solution)/shard_map/ppermute | solution.py:74
  59.8 2.2 %collective-permute-done.9 = bf16[192,4,256]{2,0,1:T(8,128)(2,1)S(1)} collective-permute-done((bf16[192,4,256]{2,0,1:T(8,128)(2,1)}, bf16[192,4,256]{2,0,1:T(8,128)(2,1)S(1)}, u32[]{:S(2)}, u32[]{:S(2)}) %collective-permute-start.9) | collective-permute-done | bytes 393248 | tf_op jit(solution)/shard_map/ppermute | solution.py:75
  64.0 3.8 %collective-permute-done.10 = bf16[192,4,256]{2,0,1:T(8,128)(2,1)} collective-permute-done((bf16[192,4,256]{2,0,1:T(8,128)(2,1)}, bf16[192,4,256]{2,0,1:T(8,128)(2,1)}, u32[]{:S(2)}, u32[]{:S(2)}) %collective-permute-start.10) | collective-permute-done | bytes 393248 | tf_op jit(solution)/shard_map/ppermute | solution.py:74
  75.3 2.4 %collective-permute-done.12 = bf16[192,4,256]{2,0,1:T(8,128)(2,1)S(1)} collective-permute-done((bf16[192,4,256]{2,0,1:T(8,128)(2,1)}, bf16[192,4,256]{2,0,1:T(8,128)(2,1)S(1)}, u32[]{:S(2)}, u32[]{:S(2)}) %collective-permute-start.12) | collective-permute-done | bytes 393248 | tf_op jit(solution)/shard_map/ppermute | solution.py:74
  85.3 2.4 %collective-permute-done.14 = bf16[192,4,256]{2,0,1:T(8,128)(2,1)S(1)} collective-permute-done((bf16[192,4,256]{2,0,1:T(8,128)(2,1)S(1)}, bf16[192,4,256]{2,0,1:T(8,128)(2,1)S(1)}, u32[]{:S(2)}, u32[]{:S(2)}) %collective-permute-start.14) | collective-permute-done | bytes 393248 | tf_op jit(solution)/shard_map/ppermute | solution.py:74
  95.3 2.4 %collective-permute-done.16 = bf16[192,4,256]{2,0,1:T(8,128)(2,1)S(1)} collective-permute-done((bf16[192,4,256]{2,0,1:T(8,128)(2,1)S(1)}, bf16[192,4,256]{2,0,1:T(8,128)(2,1)S(1)}, u32[]{:S(2)}, u32[]{:S(2)}) %collective-permute-start.16) | collective-permute-done | bytes 393248 | tf_op jit(solution)/shard_map/ppermute | solution.py:74
  104.3 3.4 %collective-permute-done.18 = bf16[192,4,256]{2,0,1:T(8,128)(2,1)S(1)} collective-permute-done((bf16[192,4,256]{2,0,1:T(8,128)(2,1)S(1)}, bf16[192,4,256]{2,0,1:T(8,128)(2,1)S(1)}, u32[]{:S(2)}, u32[]{:S(2)}) %collective-permute-start.18) | collective-permute-done | bytes 393248 | tf_op jit(solution)/shard_map/ppermute | solution.py:74
  111.9 2.1 %collective-permute-start.21 = (bf16[192,4,256]{2,0,1:T(8,128)(2,1)S(1)}, bf16[192,4,256]{2,0,1:T(8,128)(2,1)S(1)}, u32[]{:S(2)}, u32[]{:S(2)}) collective-permute-start(bf16[192,4,256]{2,0,1:T(8,128)(2,1)S(1)} %collective-permute-done.19), channel_id=1, source_target_pairs={{0,1},{1,2},{2,3},{3,4},{4,5},{5,6},{6,7},{7,8},{8,9},{9,10},{10,1... | collective-permute-start | bytes 1179656 | tf_op jit(solution)/shard_map/ppermute | solution.py:75
  114.5 3.2 %collective-permute-done.20 = bf16[192,4,256]{2,0,1:T(8,128)(2,1)S(1)} collective-permute-done((bf16[192,4,256]{2,0,1:T(8,128)(2,1)S(1)}, bf16[192,4,256]{2,0,1:T(8,128)(2,1)S(1)}, u32[]{:S(2)}, u32[]{:S(2)}) %collective-permute-start.20) | collective-permute-done | bytes 393248 | tf_op jit(solution)/shard_map/ppermute | solution.py:74
  123.8 2.6 %fusion.58 = f32[4,2,192,256]{3,2,0,1:T(8,128)} fusion(bf16[4,2,192,192]{2,3,1,0:T(8,128)(2,1)S(1)} %get-tuple-element.39, bf16[192,4,256]{2,0,1:T(8,128)(2,1)} %collective-permute-done.7), kind=kOutput, calls=%fused_computation.77 | convolution fusion | flops 150994944 | bytes 2555904 | tf_op jit(solution)/shard_map/kgts,skd->kgtd/dot_general | solution.py:41
  128.0 2.6 %fusion.60 = f32[4,2,192,256]{3,2,0,1:T(8,128)} fusion(bf16[4,2,192,192]{2,3,1,0:T(8,128)(2,1)S(1)} %get-tuple-element.37, bf16[192,4,256]{2,0,1:T(8,128)(2,1)} %collective-permute-done.5), kind=kOutput, calls=%fused_computation.79 | convolution fusion | flops 150994944 | bytes 2555904 | tf_op jit(solution)/shard_map/kgts,skd->kgtd/dot_general | solution.py:41
  130.6 2.6 %fusion.62 = f32[4,2,192,256]{3,2,0,1:T(8,128)} fusion(bf16[4,2,192,192]{2,3,1,0:T(8,128)(2,1)S(1)} %get-tuple-element.35, bf16[192,4,256]{2,0,1:T(8,128)(2,1)} %collective-permute-done.3), kind=kOutput, calls=%fused_computation.81 | convolution fusion | flops 150994944 | bytes 2555904 | tf_op jit(solution)/shard_map/kgts,skd->kgtd/dot_general | solution.py:41
  133.2 2.7 %fusion.64 = f32[4,2,192,256]{3,2,0,1:T(8,128)} fusion(bf16[4,2,192,192]{2,3,1,0:T(8,128)(2,1)S(1)} %get-tuple-element.33, bf16[192,4,256]{2,0,1:T(8,128)(2,1)} %collective-permute-done.1), kind=kOutput, calls=%fused_computation.83 | convolution fusion | flops 150994944 | bytes 2555904 | tf_op jit(solution)/shard_map/kgts,skd->kgtd/dot_general | solution.py:41
  143.4 14.5 %fusion.11 = bf16[192,2560]{1,0:T(8,128)(2,1)} fusion(bf16[4,2,256,2560]{3,2,1,0:T(8,128)(2,1)} %bitcast.187, f32[4,2,192,256]{3,2,0,1:T(8,128)} %fusion.46, f32[4,2,192,256]{3,2,0,1:T(8,128)} %fusion.48, f32[4,2,192,256]{3,2,0,1:T(8,128)} %fusion.50, f32[4,2,192,256]{3,2,0,1:T(8,128)} %fusion.52, f32[4,2,192,256]{3,2,0,1:T(8,128)} %fusion.54, ...), kind=kOutput, calls=%fused_computation.9 | convolution fusion | flops 2174582784 | bytes 29833216 | tf_op jit(solution)/shard_map/kgtd,kgde->te/dot_general | solution.py:50
  (124 shorter events, 60.7 us)
Async XLA Ops:
  0.0 8.3 %copy-start.9 = (bf16[2560,4,256]{2,1,0:T(4,128)(2,1)S(1)}, bf16[2560,4,256]{2,1,0:T(4,128)(2,1)}, u32[]{:S(2)}) copy-start(bf16[2560,4,256]{2,1,0:T(4,128)(2,1)} %param.8) | copy-start | bytes 15728644
  1.2 12.7 %slice-start = ((s8[10485760]{0:T(1024)(128)(4,1)}), s8[4194304]{0:T(1024)(128)(4,1)S(1)}, s32[]{:S(2)}) async-start(s8[10485760]{0:T(1024)(128)(4,1)} %bitcast.185), calls=%async_computation | async-start | bytes 8388608
  1.2 12.7 %slice-start.1 = ((s8[10485760]{0:T(1024)(128)(4,1)}), s8[4194304]{0:T(1024)(128)(4,1)S(1)}, s32[]{:S(2)}) async-start(s8[10485760]{0:T(1024)(128)(4,1)} %bitcast.185), calls=%async_computation.1 | async-start | bytes 8388608
  6.3 7.6 %slice-start.2 = ((s8[10485760]{0:T(1024)(128)(4,1)}), s8[2097152]{0:T(1024)(128)(4,1)S(1)}, s32[]{:S(2)}) async-start(s8[10485760]{0:T(1024)(128)(4,1)} %bitcast.185), calls=%async_computation.2 | async-start | bytes 4194304
  6.3 11.5 %collective-permute-start = (bf16[192,4,256]{2,0,1:T(8,128)(2,1)}, bf16[192,4,256]{2,0,1:T(8,128)(2,1)}, u32[]{:S(2)}, u32[]{:S(2)}) collective-permute-start(bf16[192,4,256]{2,0,1:T(8,128)(2,1)} %pad_maximum_fusion.1), channel_id=1, source_target_pairs={{0,1},{1,2},{2,3},{3,4},{4,5},{5,6},{6,7},{7,8},{8,9},{9,10},{10,1... | collective-permute-start | bytes 1179656 | tf_op jit(solution)/shard_map/ppermute | solution.py:74
  10.3 10.3 %collective-permute-start.1 = (bf16[192,4,256]{2,0,1:T(8,128)(2,1)}, bf16[192,4,256]{2,0,1:T(8,128)(2,1)}, u32[]{:S(2)}, u32[]{:S(2)}) collective-permute-start(bf16[192,4,256]{2,0,1:T(8,128)(2,1)} %fusion.38), channel_id=1, source_target_pairs={{0,1},{1,2},{2,3},{3,4},{4,5},{5,6},{6,7},{7,8},{8,9},{9,10},{10,1... | collective-permute-start | bytes 1179656 | tf_op jit(solution)/shard_map/ppermute | solution.py:75
  17.8 10.0 %collective-permute-start.2 = (bf16[192,4,256]{2,0,1:T(8,128)(2,1)}, bf16[192,4,256]{2,0,1:T(8,128)(2,1)}, u32[]{:S(2)}, u32[]{:S(2)}) collective-permute-start(bf16[192,4,256]{2,0,1:T(8,128)(2,1)} %collective-permute-done), channel_id=1, source_target_pairs={{0,1},{1,2},{2,3},{3,4},{4,5},{5,6},{6,7},{7,8},{8,9},{9,10},{10,1... | collective-permute-start | bytes 1179656 | tf_op jit(solution)/shard_map/ppermute | solution.py:74
  20.6 11.4 %collective-permute-start.3 = (bf16[192,4,256]{2,0,1:T(8,128)(2,1)}, bf16[192,4,256]{2,0,1:T(8,128)(2,1)}, u32[]{:S(2)}, u32[]{:S(2)}) collective-permute-start(bf16[192,4,256]{2,0,1:T(8,128)(2,1)} %collective-permute-done.1), channel_id=1, source_target_pairs={{0,1},{1,2},{2,3},{3,4},{4,5},{5,6},{6,7},{7,8},{8,9},{9,10},{10,1... | collective-permute-start | bytes 1179656 | tf_op jit(solution)/shard_map/ppermute | solution.py:75
  27.8 10.0 %collective-permute-start.4 = (bf16[192,4,256]{2,0,1:T(8,128)(2,1)}, bf16[192,4,256]{2,0,1:T(8,128)(2,1)}, u32[]{:S(2)}, u32[]{:S(2)}) collective-permute-start(bf16[192,4,256]{2,0,1:T(8,128)(2,1)} %collective-permute-done.2), channel_id=1, source_target_pairs={{0,1},{1,2},{2,3},{3,4},{4,5},{5,6},{6,7},{7,8},{8,9},{9,10},{10,1... | collective-permute-start | bytes 1179656 | tf_op jit(solution)/shard_map/ppermute | solution.py:74
  30.0 39.7 %copy-start.3 = (bf16[192,8,128]{2,0,1:T(8,128)(2,1)S(1)}, bf16[192,8,128]{2,0,1:T(8,128)(2,1)}, u32[]{:S(2)}) copy-start(bf16[192,8,128]{2,0,1:T(8,128)(2,1)} %copy-done.2) | copy-start | bytes 1179652
  32.0 10.0 %collective-permute-start.5 = (bf16[192,4,256]{2,0,1:T(8,128)(2,1)}, bf16[192,4,256]{2,0,1:T(8,128)(2,1)}, u32[]{:S(2)}, u32[]{:S(2)}) collective-permute-start(bf16[192,4,256]{2,0,1:T(8,128)(2,1)} %collective-permute-done.3), channel_id=1, source_target_pairs={{0,1},{1,2},{2,3},{3,4},{4,5},{5,6},{6,7},{7,8},{8,9},{9,10},{10,1... | collective-permute-start | bytes 1179656 | tf_op jit(solution)/shard_map/ppermute | solution.py:75
  37.8 10.0 %collective-permute-start.6 = (bf16[192,4,256]{2,0,1:T(8,128)(2,1)}, bf16[192,4,256]{2,0,1:T(8,128)(2,1)}, u32[]{:S(2)}, u32[]{:S(2)}) collective-permute-start(bf16[192,4,256]{2,0,1:T(8,128)(2,1)} %collective-permute-done.4), channel_id=1, source_target_pairs={{0,1},{1,2},{2,3},{3,4},{4,5},{5,6},{6,7},{7,8},{8,9},{9,10},{10,1... | collective-permute-start | bytes 1179656 | tf_op jit(solution)/shard_map/ppermute | solution.py:74
  42.0 10.0 %collective-permute-start.7 = (bf16[192,4,256]{2,0,1:T(8,128)(2,1)}, bf16[192,4,256]{2,0,1:T(8,128)(2,1)}, u32[]{:S(2)}, u32[]{:S(2)}) collective-permute-start(bf16[192,4,256]{2,0,1:T(8,128)(2,1)} %collective-permute-done.5), channel_id=1, source_target_pairs={{0,1},{1,2},{2,3},{3,4},{4,5},{5,6},{6,7},{7,8},{8,9},{9,10},{10,1... | collective-permute-start | bytes 1179656 | tf_op jit(solution)/shard_map/ppermute | solution.py:75
  47.8 10.0 %collective-permute-start.8 = (bf16[192,4,256]{2,0,1:T(8,128)(2,1)}, bf16[192,4,256]{2,0,1:T(8,128)(2,1)}, u32[]{:S(2)}, u32[]{:S(2)}) collective-permute-start(bf16[192,4,256]{2,0,1:T(8,128)(2,1)} %collective-permute-done.6), channel_id=1, source_target_pairs={{0,1},{1,2},{2,3},{3,4},{4,5},{5,6},{6,7},{7,8},{8,9},{9,10},{10,1... | collective-permute-start | bytes 1179656 | tf_op jit(solution)/shard_map/ppermute | solution.py:74
  52.0 10.0 %collective-permute-start.9 = (bf16[192,4,256]{2,0,1:T(8,128)(2,1)}, bf16[192,4,256]{2,0,1:T(8,128)(2,1)S(1)}, u32[]{:S(2)}, u32[]{:S(2)}) collective-permute-start(bf16[192,4,256]{2,0,1:T(8,128)(2,1)} %collective-permute-done.7), channel_id=1, source_target_pairs={{0,1},{1,2},{2,3},{3,4},{4,5},{5,6},{6,7},{7,8},{8,9},{9,10},{10,1... | collective-permute-start | bytes 1179656 | tf_op jit(solution)/shard_map/ppermute | solution.py:75
  57.8 10.0 %collective-permute-start.10 = (bf16[192,4,256]{2,0,1:T(8,128)(2,1)}, bf16[192,4,256]{2,0,1:T(8,128)(2,1)}, u32[]{:S(2)}, u32[]{:S(2)}) collective-permute-start(bf16[192,4,256]{2,0,1:T(8,128)(2,1)} %collective-permute-done.8), channel_id=1, source_target_pairs={{0,1},{1,2},{2,3},{3,4},{4,5},{5,6},{6,7},{7,8},{8,9},{9,10},{10,1... | collective-permute-start | bytes 1179656 | tf_op jit(solution)/shard_map/ppermute | solution.py:74
  62.0 9.1 %copy-start.4 = (bf16[192,4,256]{2,0,1:T(8,128)(2,1)}, bf16[192,4,256]{2,0,1:T(8,128)(2,1)S(1)}, u32[]{:S(2)}) copy-start(bf16[192,4,256]{2,0,1:T(8,128)(2,1)S(1)} %collective-permute-done.9) | copy-start | bytes 1179652
  62.0 10.0 %collective-permute-start.11 = (bf16[192,4,256]{2,0,1:T(8,128)(2,1)S(1)}, bf16[192,4,256]{2,0,1:T(8,128)(2,1)S(1)}, u32[]{:S(2)}, u32[]{:S(2)}) collective-permute-start(bf16[192,4,256]{2,0,1:T(8,128)(2,1)S(1)} %collective-permute-done.9), channel_id=1, source_target_pairs={{0,1},{1,2},{2,3},{3,4},{4,5},{5,6},{6,7},{7,8},{8,9},{9,10},{10,1... | collective-permute-start | bytes 1179656 | tf_op jit(solution)/shard_map/ppermute | solution.py:75
  67.8 10.0 %collective-permute-start.12 = (bf16[192,4,256]{2,0,1:T(8,128)(2,1)}, bf16[192,4,256]{2,0,1:T(8,128)(2,1)S(1)}, u32[]{:S(2)}, u32[]{:S(2)}) collective-permute-start(bf16[192,4,256]{2,0,1:T(8,128)(2,1)} %collective-permute-done.10), channel_id=1, source_target_pairs={{0,1},{1,2},{2,3},{3,4},{4,5},{5,6},{6,7},{7,8},{8,9},{9,10},{10,1... | collective-permute-start | bytes 1179656 | tf_op jit(solution)/shard_map/ppermute | solution.py:74
  72.0 10.0 %collective-permute-start.13 = (bf16[192,4,256]{2,0,1:T(8,128)(2,1)S(1)}, bf16[192,4,256]{2,0,1:T(8,128)(2,1)S(1)}, u32[]{:S(2)}, u32[]{:S(2)}) collective-permute-start(bf16[192,4,256]{2,0,1:T(8,128)(2,1)S(1)} %collective-permute-done.11), channel_id=1, source_target_pairs={{0,1},{1,2},{2,3},{3,4},{4,5},{5,6},{6,7},{7,8},{8,9},{9,10},{10,1... | collective-permute-start | bytes 1179656 | tf_op jit(solution)/shard_map/ppermute | solution.py:75
  77.8 10.0 %collective-permute-start.14 = (bf16[192,4,256]{2,0,1:T(8,128)(2,1)S(1)}, bf16[192,4,256]{2,0,1:T(8,128)(2,1)S(1)}, u32[]{:S(2)}, u32[]{:S(2)}) collective-permute-start(bf16[192,4,256]{2,0,1:T(8,128)(2,1)S(1)} %collective-permute-done.12), channel_id=1, source_target_pairs={{0,1},{1,2},{2,3},{3,4},{4,5},{5,6},{6,7},{7,8},{8,9},{9,10},{10,1... | collective-permute-start | bytes 1179656 | tf_op jit(solution)/shard_map/ppermute | solution.py:74
  81.1 8.6 %copy-start.8 = (pred[192,192]{0,1:T(8,128)(4,1)S(1)}, pred[192,192]{0,1:T(8,128)(4,1)}, u32[]{:S(2)}) copy-start(pred[192,192]{0,1:T(8,128)(4,1)} %fusion.140) | copy-start | bytes 110596
  82.0 10.0 %collective-permute-start.15 = (bf16[192,4,256]{2,0,1:T(8,128)(2,1)S(1)}, bf16[192,4,256]{2,0,1:T(8,128)(2,1)S(1)}, u32[]{:S(2)}, u32[]{:S(2)}) collective-permute-start(bf16[192,4,256]{2,0,1:T(8,128)(2,1)S(1)} %collective-permute-done.13), channel_id=1, source_target_pairs={{0,1},{1,2},{2,3},{3,4},{4,5},{5,6},{6,7},{7,8},{8,9},{9,10},{10,1... | collective-permute-start | bytes 1179656 | tf_op jit(solution)/shard_map/ppermute | solution.py:75
  85.3 8.6 %copy-start.7 = (pred[192,192]{0,1:T(8,128)(4,1)S(1)}, pred[192,192]{0,1:T(8,128)(4,1)}, u32[]{:S(2)}) copy-start(pred[192,192]{0,1:T(8,128)(4,1)} %fusion.142) | copy-start | bytes 110596
  87.7 10.0 %collective-permute-start.16 = (bf16[192,4,256]{2,0,1:T(8,128)(2,1)S(1)}, bf16[192,4,256]{2,0,1:T(8,128)(2,1)S(1)}, u32[]{:S(2)}, u32[]{:S(2)}) collective-permute-start(bf16[192,4,256]{2,0,1:T(8,128)(2,1)S(1)} %collective-permute-done.14), channel_id=1, source_target_pairs={{0,1},{1,2},{2,3},{3,4},{4,5},{5,6},{6,7},{7,8},{8,9},{9,10},{10,1... | collective-permute-start | bytes 1179656 | tf_op jit(solution)/shard_map/ppermute | solution.py:74
  91.1 8.6 %copy-start.6 = (pred[192,192]{0,1:T(8,128)(4,1)S(1)}, pred[192,192]{0,1:T(8,128)(4,1)}, u32[]{:S(2)}) copy-start(pred[192,192]{0,1:T(8,128)(4,1)} %fusion.144) | copy-start | bytes 110596
  92.0 10.0 %collective-permute-start.17 = (bf16[192,4,256]{2,0,1:T(8,128)(2,1)S(1)}, bf16[192,4,256]{2,0,1:T(8,128)(2,1)S(1)}, u32[]{:S(2)}, u32[]{:S(2)}) collective-permute-start(bf16[192,4,256]{2,0,1:T(8,128)(2,1)S(1)} %collective-permute-done.15), channel_id=1, source_target_pairs={{0,1},{1,2},{2,3},{3,4},{4,5},{5,6},{6,7},{7,8},{8,9},{9,10},{10,1... | collective-permute-start | bytes 1179656 | tf_op jit(solution)/shard_map/ppermute | solution.py:75
  97.7 10.0 %collective-permute-start.18 = (bf16[192,4,256]{2,0,1:T(8,128)(2,1)S(1)}, bf16[192,4,256]{2,0,1:T(8,128)(2,1)S(1)}, u32[]{:S(2)}, u32[]{:S(2)}) collective-permute-start(bf16[192,4,256]{2,0,1:T(8,128)(2,1)S(1)} %collective-permute-done.16), channel_id=1, source_target_pairs={{0,1},{1,2},{2,3},{3,4},{4,5},{5,6},{6,7},{7,8},{8,9},{9,10},{10,1... | collective-permute-start | bytes 1179656 | tf_op jit(solution)/shard_map/ppermute | solution.py:74
  101.9 10.0 %collective-permute-start.19 = (bf16[192,4,256]{2,0,1:T(8,128)(2,1)S(1)}, bf16[192,4,256]{2,0,1:T(8,128)(2,1)S(1)}, u32[]{:S(2)}, u32[]{:S(2)}) collective-permute-start(bf16[192,4,256]{2,0,1:T(8,128)(2,1)S(1)} %collective-permute-done.17), channel_id=1, source_target_pairs={{0,1},{1,2},{2,3},{3,4},{4,5},{5,6},{6,7},{7,8},{8,9},{9,10},{10,1... | collective-permute-start | bytes 1179656 | tf_op jit(solution)/shard_map/ppermute | solution.py:75
  107.7 10.0 %collective-permute-start.20 = (bf16[192,4,256]{2,0,1:T(8,128)(2,1)S(1)}, bf16[192,4,256]{2,0,1:T(8,128)(2,1)S(1)}, u32[]{:S(2)}, u32[]{:S(2)}) collective-permute-start(bf16[192,4,256]{2,0,1:T(8,128)(2,1)S(1)} %collective-permute-done.18), channel_id=1, source_target_pairs={{0,1},{1,2},{2,3},{3,4},{4,5},{5,6},{6,7},{7,8},{8,9},{9,10},{10,1... | collective-permute-start | bytes 1179656 | tf_op jit(solution)/shard_map/ppermute | solution.py:74
  111.9 30.8 %collective-permute-start.21 = (bf16[192,4,256]{2,0,1:T(8,128)(2,1)S(1)}, bf16[192,4,256]{2,0,1:T(8,128)(2,1)S(1)}, u32[]{:S(2)}, u32[]{:S(2)}) collective-permute-start(bf16[192,4,256]{2,0,1:T(8,128)(2,1)S(1)} %collective-permute-done.19), channel_id=1, source_target_pairs={{0,1},{1,2},{2,3},{3,4},{4,5},{5,6},{6,7},{7,8},{8,9},{9,10},{10,1... | collective-permute-start | bytes 1179656 | tf_op jit(solution)/shard_map/ppermute | solution.py:75
  143.4 14.5 %copy-start.1 = (bf16[192,2560]{1,0:T(8,128)(2,1)S(1)}, bf16[192,2560]{1,0:T(8,128)(2,1)}, u32[]{:S(2)}) copy-start(bf16[192,2560]{1,0:T(8,128)(2,1)} %param.5) | copy-start | bytes 2949124
  (4 other events, 4.4 us)
where the time goes:
time: 159 us; the launch traced here: 158 us
  matrix products  55.6 us (35%)
  waiting for transfers between devices  47.5 us (30%)
  starting transfers between devices  43.9 us (28%)
  other arithmetic  7.87 us (5%)
  local copies, waits for them, and re-layouts  2.28 us (1%)
    ppermute x11, waiting for transfers between devices, local_fn(): k_cur = lax.ppermute(k_cur, ('cpo', 'cpi'), shift_perm)  33.8 us
    ppermute x11, starting transfers between devices, local_fn(): v_cur = lax.ppermute(v_cur, ('cpo', 'cpi'), shift_perm)  22.8 us
    dot_general x11, matrix products, attend_step(): jnp.einsum('kgts,skd->kgtd', exp_scores.astype(jnp.bfloat16), v_blk, pref...  21.7 us
    ppermute x11, starting transfers between devices, local_fn(): k_cur = lax.ppermute(k_cur, ('cpo', 'cpi'), shift_perm)  21.1 us
    dot_general x1, matrix products, finish_output(): jnp.einsum('kgtd,kgde->te', attended, w_grp, preferred_element_type=jnp.f...  14.5 us
    ppermute x11, waiting for transfers between devices, local_fn(): v_cur = lax.ppermute(v_cur, ('cpo', 'cpi'), shift_perm)  13.7 us
    dot_general x12, matrix products, attend_step(): jnp.einsum('tkgd,skd->kgts', q_grp, k_blk, preferred_element_type=jnp.flo...  11.1 us
    dot_general x1, matrix products, project_local(): jnp.einsum('td,dhe->the', hidden, w_k, preferred_element_type=jnp.float32)  4.2 us
  transfers between devices with their start and end apart: 22, of which 20 were waited for; matrix products, arithmetic and copies ran while one was open for 28% of the time, Pallas kernels for 0%

commit v1 on v0

v1 whole, which is shorter than its diff:
```python
import functools

import jax
import jax.numpy as jnp
from jax import lax
from jax.experimental import pallas as pl
from jax.experimental.pallas import tpu as pltpu
from jax.sharding import PartitionSpec as P

WINDOW = 2048
ROPE_BASE = 10000.0
MESH = pl.DeviceIdType.MESH
NL = 4
TOK = 192
LVL = NL * TOK
HD = 256
ROWS = 2 * TOK
CHUNK = 256
NEG = -1e30
LOG2E = 1.4426950408889634


def rope(vals, pos):
    half = vals.shape[-1] // 2
    inv_freq = ROPE_BASE ** (-jnp.arange(half, dtype=jnp.float32) * 2.0 / vals.shape[-1])
    ang = pos.astype(jnp.float32)[:, None] * inv_freq
    c, s = jnp.cos(ang)[None], jnp.sin(ang)[None]
    lo, hi = vals[..., :half], vals[..., half:]
    return jnp.concatenate([lo * c - hi * s, hi * c + lo * s], axis=-1).astype(jnp.bfloat16)


def body(q_ref, k_ref, v_ref, wo_hbm, y_ref, kb, vb, qb, ob, osend, acc, m_s, l_s, wo,
         krecv, vrecv, kfs, vfs, ksend, vsend, qsend, qrecv, os_sem, orecv, wsem):
    d, a, b = lax.axis_index("dp"), lax.axis_index("cpo"), lax.axis_index("cpi")
    shard = a * NL + b

    wcopy = pltpu.make_async_copy(wo_hbm, wo, wsem)
    wcopy.start()

    bar = pltpu.get_barrier_semaphore()
    for step in range(1, NL):
        pl.semaphore_signal(bar, inc=1, device_id=(d, a, lax.rem(b + step, NL)), device_id_type=MESH)

    @pl.when(a > 0)
    def _():
        pl.semaphore_signal(bar, inc=1, device_id=(d, a - 1, b), device_id_type=MESH)

    @pl.when(a < NL - 1)
    def _():
        pl.semaphore_signal(bar, inc=1, device_id=(d, a + 1, b), device_id_type=MESH)

    ends = (a == 0).astype(jnp.int32) + (a == NL - 1).astype(jnp.int32)
    pl.semaphore_wait(bar, NL + 1 - ends)

    def rows(s):
        return pl.ds(pl.multiple_of(s * TOK, TOK), TOK)

    def remote(src, dst, ss, rs, dev):
        return pltpu.make_async_remote_copy(src_ref=src, dst_ref=dst, send_sem=ss, recv_sem=rs,
                                            device_id=dev, device_id_type=MESH)

    def exchange(h, what):
        dev = (d, a, h)
        if what == "k":
            return remote(k_ref.at[h], kb.at[rows(shard)], ksend.at[h], krecv.at[shard], dev)
        if what == "v":
            return remote(v_ref.at[h], vb.at[rows(shard)], vsend.at[h], vrecv.at[shard], dev)
        return remote(q_ref.at[h], qb.at[b], qsend.at[h], qrecv.at[b], dev)

    for what in ("k", "v", "q"):
        for h in range(NL):
            @pl.when(b != h)
            def _():
                exchange(h, what).start()

    kb[rows(shard), :] = k_ref[b]
    vb[rows(shard), :] = v_ref[b]
    qb[b] = q_ref[b]

    def forward(s):
        dev = (d, a + 1, b)
        return (remote(kb.at[rows(s)], kb.at[rows(s)], kfs.at[s], krecv.at[s], dev),
                remote(vb.at[rows(s)], vb.at[rows(s)], vfs.at[s], vrecv.at[s], dev))

    def wait_piece(s):
        forwarded = forward(s)
        forwarded[0].wait_recv()
        forwarded[1].wait_recv()

    def needed(s, level):
        return s >= NL * level - 11

    def pass_on(s):
        @pl.when((a < NL - 1) & needed(s, a + 1))
        def _():
            for c in forward(s):
                c.start()

    pass_on(shard)
    partner = b + 1 - 2 * lax.rem(b, 2)
    far = lax.rem(b + 2, NL)
    far2 = lax.rem(partner + 2, NL)
    for j in (partner, far, far2):
        s = a * NL + j
        wait_piece(s)
        pass_on(s)

    for j in (partner, far, far2):
        remote(q_ref.at[0], qb.at[j], qsend.at[0], qrecv.at[j], (d, a, b)).wait_recv()

    def attend(i, key0, masked, first):
        q = qb[i].reshape(ROWS, HD)
        keys = pl.ds(pl.multiple_of(key0, CHUNK), CHUNK)
        s = lax.dot_general(q, kb[keys, :], (((1,), (1,)), ((), ())), preferred_element_type=jnp.float32)
        if masked:
            row = lax.broadcasted_iota(jnp.int32, (2, TOK, CHUNK), 1).reshape(ROWS, CHUNK)
            col = lax.broadcasted_iota(jnp.int32, (ROWS, CHUNK), 1)
            gap = row - col + (a * LVL + i * TOK - key0)
            s = jnp.where((gap >= 0) & (gap < WINDOW), s, NEG)
        top = jnp.max(s, axis=-1, keepdims=True)
        old = m_s[i]
        new = jnp.maximum(old, top)
        scale = HD ** -0.5 * LOG2E
        p = jnp.exp2((s - new) * scale)
        fix = jnp.exp2((old - new) * scale)
        l_s[i] = l_s[i] * fix + jnp.sum(p, axis=-1, keepdims=True)
        acc[i] = acc[i] * fix + jnp.dot(p.astype(jnp.bfloat16), vb[keys, :], preferred_element_type=jnp.float32)
        m_s[i] = new

    m_s[...] = jnp.full_like(m_s, NEG)
    l_s[...] = jnp.zeros_like(l_s)
    acc[...] = jnp.zeros_like(acc)

    def own(i, carry):
        n = lax.div(i * TOK + TOK + CHUNK - 1, CHUNK)

        def one(c, carry):
            attend(i, a * LVL + c * CHUNK, True, False)
            return carry

        return lax.fori_loop(0, n, one, carry)

    lax.fori_loop(0, NL, own, 0)

    for back in (1, 2, 3):
        @pl.when(a >= back)
        def _():
            base = (a - back) * NL
            for j in range(NL):
                @pl.when(needed(base + j, a))
                def _():
                    wait_piece(base + j)
                    pass_on(base + j)

            first = 1 if back == 3 else 0
            last = NL - 1 if back == 3 else NL

            def over(i, carry):
                def one(c, carry):
                    attend(i, base * TOK + c * CHUNK, back > 1, False)
                    return carry
                return lax.fori_loop(first, LVL // CHUNK, one, carry)

            lax.fori_loop(0, last, over, 0)

    def back_to(i):
        cols = pl.ds(pl.multiple_of(b * 2 * HD, 2 * HD), 2 * HD)
        return remote(osend.at[i], ob.at[:, cols], os_sem.at[i], orecv.at[b], (d, a, i))

    for i in range(NL):
        o = (acc[i] / l_s[i]).astype(jnp.bfloat16)
        osend[i] = jnp.concatenate([o[:TOK], o[TOK:]], axis=1)

        @pl.when(b != i)
        def _():
            back_to(i).start()

    for h in range(NL):
        cols = pl.ds(h * 2 * HD, 2 * HD)

        @pl.when(b == h)
        def _():
            ob[:, cols] = osend[h]

        @pl.when(b != h)
        def _():
            remote(osend.at[0], ob.at[:, cols], os_sem.at[0], orecv.at[h], (d, a, b)).wait_recv()

    wcopy.wait()
    y_ref[...] = jnp.dot(ob[...], wo[...], preferred_element_type=jnp.float32).astype(jnp.bfloat16)

    for i in range(NL):
        @pl.when(b != i)
        def _():
            back_to(i).wait_send()
            for what in ("k", "v", "q"):
                exchange(i, what).wait_send()

    for s in range(12):
        @pl.when((a < NL - 1) & (s < NL * (a + 1)) & needed(s, a + 1))
        def _():
            for c in forward(s):
                c.wait_send()


def solution(mesh):
    def local_fn(hidden, w_q, w_k, w_v, w_o):
        shard = lax.axis_index("cpo") * NL + lax.axis_index("cpi")
        pos = shard * TOK + jnp.arange(TOK)
        k = rope(jnp.einsum("td,dhe->hte", hidden, w_k, preferred_element_type=jnp.float32), pos)
        v = jnp.einsum("td,dhe->hte", hidden, w_v, preferred_element_type=jnp.float32).astype(jnp.bfloat16)
        q = rope(jnp.einsum("td,dhe->hte", hidden, w_q, preferred_element_type=jnp.float32), pos)
        q = q.reshape(NL, 2, TOK, HD)
        vm = pl.BlockSpec(memory_space=pltpu.VMEM)
        dma = pltpu.SemaphoreType.DMA
        bf, f32 = jnp.bfloat16, jnp.float32
        return pl.pallas_call(
            body,
            out_shape=jax.ShapeDtypeStruct((TOK, 2560), bf),
            in_specs=[vm, vm, vm, pl.BlockSpec(memory_space=pl.ANY)],
            out_specs=vm,
            scratch_shapes=[
                pltpu.VMEM((16 * TOK, HD), bf), pltpu.VMEM((16 * TOK, HD), bf),
                pltpu.VMEM((NL, 2, TOK, HD), bf), pltpu.VMEM((TOK, 8 * HD), bf),
                pltpu.VMEM((NL, TOK, 2 * HD), bf), pltpu.VMEM((NL, ROWS, HD), f32),
                pltpu.VMEM((NL, ROWS, 1), f32), pltpu.VMEM((NL, ROWS, 1), f32),
                pltpu.VMEM((8 * HD, 2560), bf),
                dma((16,)), dma((16,)), dma((16,)), dma((16,)),
                dma((NL,)), dma((NL,)), dma((NL,)), dma((NL,)), dma((NL,)), dma((NL,)), dma(()),
            ],
            compiler_params=pltpu.CompilerParams(collective_id=0, has_side_effects=True,
                                                 vmem_limit_bytes=50 * 2 ** 20),
        )(q, k, v, w_o.reshape(8 * HD, 2560))

    return jax.shard_map(local_fn, mesh=mesh,
                         in_specs=(P(("dp", "cpo", "cpi"), None), P(), P(), P(), P()),
                         out_specs=P(("dp", "cpo", "cpi"), None), check_vma=False)
```

time: 159 us -> 87.7 us (0.55)
  the two profiles are of different devices: /device:TPU:26 before, /device:TPU:31 now
where the time goes in v1:
time: 87.7 us; the launch traced here: 87.5 us
  Pallas kernels  73.1 us (83%)
  matrix products  11.2 us (13%)
  local copies, waits for them, and re-layouts  2.16 us (2%)
  other arithmetic  0.9 us (1%)
    pallas_call x1, Pallas kernels, local_fn(): pl.pallas_call(body, out_shape=jax.ShapeDtypeStruct((TOK, 2560), bf), in_...  73.1 us
    dot_general x1, matrix products, local_fn(): jnp.einsum('td,dhe->hte', hidden, w_q, preferred_element_type=jnp.float32)  6.21 us
    dot_general x1, matrix products, local_fn(): jnp.einsum('td,dhe->hte', hidden, w_k, preferred_element_type=jnp.float32)  3.82 us
    unnamed x7, local copies, waits for them, and re-layouts  2.16 us

profile of v1, /device:TPU:31, one launch (start us, length us, event | category | flops | bytes accessed | tf_op | source)
XLA Modules:
  0.0 87.5 jit_solution(5343432422135583747)
XLA Ops:
  0.0 0.0 copy-start
  0.0 1.2 %copy-done = bf16[192,2560]{1,0:T(8,128)(2,1)S(1)} copy-done((bf16[192,2560]{1,0:T(8,128)(2,1)S(1)}, bf16[192,2560]{1,0:T(8,128)(2,1)}, u32[]{:S(2)}) %copy-start) | copy-done | bytes 983064
  1.2 6.2 %fusion.6 = f32[8,192,256]{2,1,0:T(8,128)S(1)} fusion(bf16[2560,8,256]{2,1,0:T(8,128)(2,1)} %param.6, bf16[192,2560]{1,0:T(8,128)(2,1)S(1)} %copy-done), kind=kOutput, calls=%fused_computation.6 | convolution fusion | flops 2013265920 | bytes 13041664 | tf_op jit(solution)/shard_map/td,dhe->hte/dot_general | solution.py:212
  7.5 0.4 multiply_cosine_fusion
  7.9 0.2 subtract_convert_fusion
  8.1 0.0 slice-start
  8.1 0.1 pad_maximum_fusion.q_ref
  8.2 0.0 slice-start.1
  8.2 3.8 %fusion.9 = f32[4,192,256]{2,1,0:T(8,128)S(1)} fusion(bf16[2560,4,256]{2,1,0:T(4,128)(2,1)} %param.7, bf16[192,2560]{1,0:T(8,128)(2,1)S(1)} %copy-done), kind=kOutput, calls=%fused_computation.7 | convolution fusion | flops 1006632960 | bytes 7012352 | tf_op jit(solution)/shard_map/td,dhe->hte/dot_general | solution.py:210
  12.1 0.1 subtract_convert_fusion.1
  12.2 0.0 slice-done
  12.2 0.0 slice-done.1
  12.3 1.2 %fusion.15.v_ref = bf16[4,192,256]{2,1,0:T(8,128)(2,1)S(1)} fusion(bf16[2560,4,256]{2,1,0:T(4,128)(2,1)S(1)} %bitcast.20, bf16[192,2560]{1,0:T(8,128)(2,1)S(1)} %copy-done), kind=kOutput, calls=%fused_computation.9 | convolution fusion | flops 1006829568 | bytes 6619136 | tf_op jit(solution)/shard_map/td,dhe->hte/dot_general | solution.py:211
  13.5 73.1 %shard_map.55 = bf16[192,2560]{1,0:T(8,128)(2,1)S(1)} custom-call(bf16[4,2,192,256]{3,2,1,0:T(8,128)(2,1)S(1)} %pad_maximum_fusion.q_ref, bf16[4,192,256]{2,1,0:T(8,128)(2,1)S(1)} %pad_maximum_fusion.1.k_ref, bf16[4,192,256]{2,1,0:T(8,128)(2,1)S(1)} %fusion.15.v_ref, bf16[2048,2560]{1,0:T(8,128)(2,1)} %bitcast.16), custom_call_target="tpu_custom_call" | custom-call | tf_op jit(solution)/shard_map/pallas_call | solution.py:217
  86.5 0.9 %copy.24 = bf16[192,2560]{1,0:T(8,128)(2,1)} copy(bf16[192,2560]{1,0:T(8,128)(2,1)S(1)} %shard_map.55) | data formatting | bytes 1966080
  (4 shorter events, 0.1 us)
Async XLA Ops:
  0.0 1.2 %copy-start = (bf16[192,2560]{1,0:T(8,128)(2,1)S(1)}, bf16[192,2560]{1,0:T(8,128)(2,1)}, u32[]{:S(2)}) copy-start(bf16[192,2560]{1,0:T(8,128)(2,1)} %param.5) | copy-start | bytes 2949124
  8.1 4.1 %slice-start = ((s8[5242880]{0:T(1024)(128)(4,1)}), s8[4194304]{0:T(1024)(128)(4,1)S(1)}, s32[]{:S(2)}) async-start(s8[5242880]{0:T(1024)(128)(4,1)} %bitcast.19), calls=%async_computation | async-start | bytes 8388608
  8.2 4.0 %slice-start.1 = ((s8[5242880]{0:T(1024)(128)(4,1)}), s8[1048576]{0:T(1024)(128)(4,1)S(1)}, s32[]{:S(2)}) async-start(s8[5242880]{0:T(1024)(128)(4,1)} %bitcast.19), calls=%async_computation.1 | async-start | bytes 2097152

commit v2 on v0

v2 whole, which is shorter than its diff:
```python
import jax
import jax.numpy as jnp
from jax import lax
from jax.experimental import pallas as pl
from jax.experimental.pallas import tpu as pltpu
from jax.sharding import PartitionSpec as P

WINDOW = 2048
ROPE_BASE = 10000.0
MESH = pl.DeviceIdType.MESH
NL = 4
TOK = 192
LVL = NL * TOK
DM = 2560
HD = 256
HALF = HD // 2
NEG = -1e30
SCALE = HD ** -0.5 * 1.4426950408889634
KCUT = 2
QCUT = 4
OWN_KEYS = (256, 384, 640, 768)
F32, BF = jnp.float32, jnp.bfloat16


def body(freq_ref, x_hbm, wq_hbm, wk_hbm, wv_hbm, wo_hbm, y_ref,
         x, wq, wk, wv, wo, ko, vo, qo, kb, vb, qb, ob, osend, acc, m_s, l_s,
         xsem, wksem, wvsem, wqsem, wosem, krecv, vrecv, kfs, vfs, ksend, vsend, qsend, qrecv,
         os_sem, orecv, go):
    d, a, b = lax.axis_index("dp"), lax.axis_index("cpo"), lax.axis_index("cpi")
    shard = a * NL + b
    odd = lax.rem(b, 2)
    even = odd == 0
    partner = b + 1 - 2 * odd
    far = lax.rem(b + 2, NL)
    far2 = lax.rem(partner + 2, NL)
    donor = (a == 3) & even
    host = (a == 2) & even
    feeds = (a < 2) | ((a == 2) & (odd == 1))

    def cut(src, dst, sem, n, c):
        r = DM // n
        return pltpu.make_async_copy(src.at[pl.ds(c * r, r)], dst.at[pl.ds(c * r, r)], sem.at[c])

    xcopy = pltpu.make_async_copy(x_hbm, x, xsem)
    xcopy.start()
    for c in range(KCUT):
        cut(wk_hbm, wk, wksem, KCUT, c).start()
    for c in range(KCUT):
        cut(wv_hbm, wv, wvsem, KCUT, c).start()

    bar = pltpu.get_barrier_semaphore()

    def greet(level, other):
        pl.semaphore_signal(bar, inc=1, device_id=(d, level, other), device_id_type=MESH)

    for j in (partner, far, far2):
        greet(a, j)

    @pl.when(a > 0)
    def _():
        greet(a - 1, b)

    @pl.when(a < NL - 1)
    def _():
        greet(a + 1, b)

    @pl.when(host)
    def _():
        for j in (partner, far, far2):
            greet(3, j)

    @pl.when(a == 3)
    def _():
        greet(2, lax.rem(b + 2 - odd, NL))

    @pl.when((a == 3) & (odd == 1))
    def _():
        greet(2, b - 1)

    def one(p):
        return p.astype(jnp.int32)

    pos = (lax.broadcasted_iota(jnp.int32, (TOK, HALF), 0) + shard * TOK).astype(F32)
    ang = pos * freq_ref[...]
    cos, sin = jnp.cos(ang), jnp.sin(ang)

    def project(w, n, copies, heads):
        total = None
        for c in range(n):
            copies[c].wait()
            r = DM // n
            part = jnp.dot(x[:, c * r:(c + 1) * r], w[pl.ds(c * r, r)].reshape(r, heads * HD),
                           preferred_element_type=F32)
            total = part if total is None else total + part
        return total

    def rotate(t, h):
        lo, hi = t[:, h * HD:h * HD + HALF], t[:, h * HD + HALF:(h + 1) * HD]
        return (lo * cos - hi * sin).astype(BF), (hi * cos + lo * sin).astype(BF)

    def rows(s):
        return pl.ds(pl.multiple_of(s * TOK, TOK), TOK)

    def remote(src, dst, ss, rs, dev):
        return pltpu.make_async_remote_copy(src_ref=src, dst_ref=dst, send_sem=ss, recv_sem=rs,
                                            device_id=dev, device_id_type=MESH)

    def holder(h):
        return jnp.minimum(a, 2) if h % 2 == 0 else a

    def mine(h):
        return (b == h) & (holder(h) == a)

    def exchange(h, what):
        dev = (d, holder(h), h)
        if what == "k":
            return remote(ko.at[h], kb.at[rows(shard)], ksend.at[h], krecv.at[shard], dev)
        if what == "v":
            return remote(vo.at[h], vb.at[rows(shard)], vsend.at[h], vrecv.at[shard], dev)
        slot = one(a == 3) if h % 2 == 0 else 0
        return remote(qo.at[h], qb.at[slot, b], qsend.at[h], qrecv.at[slot, b], dev)

    def send_all(what):
        for h in (0, 2, 1, 3):
            @pl.when(jnp.logical_not(mine(h)))
            def _():
                exchange(h, what).start()

    def up(s, what):
        dev = (d, a + 1, b)
        if what == "k":
            return remote(kb.at[rows(s)], kb.at[rows(s)], kfs.at[s], krecv.at[s], dev)
        return remote(vb.at[rows(s)], vb.at[rows(s)], vfs.at[s], vrecv.at[s], dev)

    def wait_piece(s):
        up(s, "k").wait_recv()
        up(s, "v").wait_recv()

    def needed(s, level):
        return s >= NL * level - 11

    def pass_on(s):
        @pl.when(feeds & needed(s, a + 1))
        def _():
            up(s, "k").start()
            up(s, "v").start()

    xcopy.wait()
    k_f = project(wk, KCUT, [cut(wk_hbm, wk, wksem, KCUT, c) for c in range(KCUT)], NL)
    for c in range(QCUT):
        cut(wq_hbm, wq, wqsem, QCUT, c).start()
    wo_copy = pltpu.make_async_copy(wo_hbm, wo, wosem)
    wo_copy.start()
    for h in range(NL):
        ko[h, :, :HALF], ko[h, :, HALF:] = rotate(k_f, h)

    @pl.when(jnp.logical_not(donor))
    def _():
        kb[rows(shard), :] = ko[b]

    pl.semaphore_wait(bar, 3 + one(a > 0) + one(a < NL - 1) + 3 * one(host) + one(a == 3) + one((a == 3) & (odd == 1)))
    send_all("k")
    v_f = project(wv, KCUT, [cut(wv_hbm, wv, wvsem, KCUT, c) for c in range(KCUT)], NL)
    for h in range(NL):
        vo[h] = v_f[:, h * HD:(h + 1) * HD].astype(BF)

    @pl.when(jnp.logical_not(donor))
    def _():
        vb[rows(shard), :] = vo[b]

    send_all("v")

    @pl.when(even)
    def _():
        pass_on(shard)

    q_f = project(wq, QCUT, [cut(wq_hbm, wq, wqsem, QCUT, c) for c in range(QCUT)], 2 * NL)
    for h in range(2 * NL):
        qo[h // 2, h % 2, :, :HALF], qo[h // 2, h % 2, :, HALF:] = rotate(q_f, h)

    @pl.when(jnp.logical_not(donor))
    def _():
        qb[0, b] = qo[b]

    send_all("q")

    @pl.when((odd == 1) & (a < 2))
    def _():
        pl.semaphore_wait(go, 1)

    def attend(slot, i, level, key0, n, masked, first):
        keys = pl.ds(pl.multiple_of(key0, 64), n)
        k, v = kb[keys, :], vb[keys, :]
        scores = []
        for g in range(2):
            s = lax.dot_general(qb[slot, i, g], k, (((1,), (1,)), ((), ())), preferred_element_type=F32)
            if masked:
                gap = (lax.broadcasted_iota(jnp.int32, (TOK, n), 0) - lax.broadcasted_iota(jnp.int32, (TOK, n), 1)
                       + (level * LVL + i * TOK - key0))
                s = jnp.where((gap >= 0) & (gap < WINDOW), s, NEG)
            scores.append(s)
        for g in range(2):
            s = scores[g]
            top = jnp.max(s, axis=-1, keepdims=True)
            if first:
                new = top
            else:
                old = m_s[i, g]
                new = jnp.maximum(old, top)
                fix = jnp.exp2((old - new) * SCALE)
            p = jnp.exp2((s - new) * SCALE)
            total = jnp.sum(p, axis=-1, keepdims=True)
            out = jnp.dot(p.astype(BF), v, preferred_element_type=F32)
            if not first:
                total = total + l_s[i, g] * fix
                out = out + acc[i, g] * fix
            m_s[i, g] = new
            l_s[i, g] = total
            acc[i, g] = out

    def attend_shards(lo, hi, fn):
        def step(i, carry):
            fn(i)
            return carry
        lax.fori_loop(lo, hi, step, 0)

    def back_to(slot, i):
        cols = pl.ds(pl.multiple_of(b * 2 * HD, 2 * HD), 2 * HD)
        return remote(osend.at[slot, i], ob.at[:, cols], os_sem.at[slot, i], orecv.at[b], (d, a + slot, i))

    def finish(slot, i):
        for g in range(2):
            osend[slot, i, :, g * HD:(g + 1) * HD] = (acc[i, g] / l_s[i, g]).astype(BF)

    @pl.when(jnp.logical_not(donor))
    def _():
        @pl.when(odd == 1)
        def _():
            pass_on(shard)

        for j in (partner, far, far2):
            wait_piece(a * NL + j)
            pass_on(a * NL + j)

        @pl.when(even & (a == 0))
        def _():
            pl.semaphore_signal(go, inc=1, device_id=(d, a, partner), device_id_type=MESH)

        for j in (partner, far, far2):
            remote(qo.at[0], qb.at[0, j], qsend.at[0], qrecv.at[0, j], (d, a, b)).wait_recv()

        for i in range(NL):
            attend(0, i, a, a * LVL, OWN_KEYS[i], True, True)

        for back in (1, 2, 3):
            @pl.when(a >= back)
            def _():
                base = (a - back) * NL
                near = b // 2 * 2
                away = 2 - near

                def take(s):
                    @pl.when(needed(s, a))
                    def _():
                        wait_piece(s)
                        pass_on(s)

                if back == 1:
                    for j in (b, partner, far, far2):
                        take(base + j)

                    @pl.when(even & (a == 1))
                    def _():
                        pl.semaphore_signal(go, inc=1, device_id=(d, a, partner), device_id_type=MESH)

                    attend_shards(0, NL, lambda i: attend(0, i, a, base * TOK, LVL, False, False))
                elif back == 2:
                    take(base + b)
                    take(base + partner)
                    attend_shards(0, NL, lambda i: attend(0, i, a, (base + near) * TOK, 2 * TOK, True, False))
                    take(base + far)
                    take(base + far2)
                    attend_shards(0, NL, lambda i: attend(0, i, a, (base + away) * TOK, 2 * TOK, True, False))
                else:
                    for j in (b, partner, far, far2):
                        take(base + j)
                    attend_shards(0, NL - 1, lambda i: attend(0, i, a, base * TOK + 256, 512, True, False))

        for i in range(NL):
            finish(0, i)

            @pl.when(b != i)
            def _():
                back_to(0, i).start()

            @pl.when(b == i)
            def _():
                ob[:, pl.ds(pl.multiple_of(b * 2 * HD, 2 * HD), 2 * HD)] = osend[0, i]

    @pl.when(host)
    def _():
        for j in range(NL):
            wait_piece(3 * NL + j)
        for j in range(NL):
            remote(qo.at[0], qb.at[1, j], qsend.at[0], qrecv.at[1, j], (d, a, b)).wait_recv()
        for i in range(NL):
            attend(1, i, 3, 3 * LVL, OWN_KEYS[i], True, True)
            attend(1, i, 3, 2 * LVL, LVL, False, False)
            attend(1, i, 3, LVL, LVL, True, False)
            if i < NL - 1:
                attend(1, i, 3, 256, 512, True, False)
            finish(1, i)
            back_to(1, i).start()

    def take_o(h):
        @pl.when(jnp.logical_not(mine(h)))
        def _():
            remote(osend.at[0, 0], ob.at[:, pl.ds(h * 2 * HD, 2 * HD)], os_sem.at[0, 0], orecv.at[h], (d, a, b)).wait_recv()

    def project_o(h):
        return jnp.dot(ob[:, h * 2 * HD:(h + 1) * 2 * HD], wo[pl.ds(h * 2 * HD, 2 * HD), :],
                       preferred_element_type=F32)

    take_o(0)
    take_o(2)
    wo_copy.wait()
    y = project_o(0) + project_o(2)
    take_o(1)
    take_o(3)
    y_ref[...] = (y + project_o(1) + project_o(3)).astype(BF)

    for h in range(NL):
        @pl.when(jnp.logical_not(mine(h)))
        def _():
            for what in ("k", "v", "q"):
                exchange(h, what).wait_send()

        @pl.when((b != h) & jnp.logical_not(donor))
        def _():
            back_to(0, h).wait_send()

        @pl.when(host)
        def _():
            back_to(1, h).wait_send()

    for s in range(12):
        @pl.when(feeds & (s < NL * (a + 1)) & needed(s, a + 1))
        def _():
            up(s, "k").wait_send()
            up(s, "v").wait_send()


def solution(mesh):
    def local_fn(hidden, w_q, w_k, w_v, w_o):
        freq = (ROPE_BASE ** (-jnp.arange(HALF, dtype=F32) * 2.0 / HD)).reshape(1, HALF)
        vm, hbm = pl.BlockSpec(memory_space=pltpu.VMEM), pl.BlockSpec(memory_space=pl.ANY)
        dma = pltpu.SemaphoreType.DMA
        return pl.pallas_call(
            body,
            out_shape=jax.ShapeDtypeStruct((TOK, DM), BF),
            in_specs=[vm, hbm, hbm, hbm, hbm, hbm],
            out_specs=vm,
            scratch_shapes=[
                pltpu.VMEM((TOK, DM), BF), pltpu.VMEM((DM, 2 * NL, HD), BF), pltpu.VMEM((DM, NL, HD), BF),
                pltpu.VMEM((DM, NL, HD), BF), pltpu.VMEM((2 * NL * HD, DM), BF),
                pltpu.VMEM((NL, TOK, HD), BF), pltpu.VMEM((NL, TOK, HD), BF), pltpu.VMEM((NL, 2, TOK, HD), BF),
                pltpu.VMEM((16 * TOK, HD), BF), pltpu.VMEM((16 * TOK, HD), BF),
                pltpu.VMEM((2, NL, 2, TOK, HD), BF), pltpu.VMEM((TOK, 2 * NL * HD), BF),
                pltpu.VMEM((2, NL, TOK, 2 * HD), BF), pltpu.VMEM((NL, 2, TOK, HD), F32),
                pltpu.VMEM((NL, 2, TOK, 1), F32), pltpu.VMEM((NL, 2, TOK, 1), F32),
                dma(()), dma((KCUT,)), dma((KCUT,)), dma((QCUT,)), dma(()),
                dma((16,)), dma((16,)), dma((16,)), dma((16,)),
                dma((NL,)), dma((NL,)), dma((NL,)), dma((2, NL)), dma((2, NL)), dma((NL,)),
                pltpu.SemaphoreType.REGULAR,
            ],
            compiler_params=pltpu.CompilerParams(collective_id=0, has_side_effects=True,
                                                 vmem_limit_bytes=63 * 2 ** 20),
        )(freq, hidden, w_q, w_k, w_v, w_o.reshape(2 * NL * HD, DM))

    return jax.shard_map(local_fn, mesh=mesh,
                         in_specs=(P(("dp", "cpo", "cpi"), None), P(), P(), P(), P()),
                         out_specs=P(("dp", "cpo", "cpi"), None), check_vma=False)
```

time: 159 us -> 75.7 us (0.48)
  the two profiles are of different devices: /device:TPU:26 before, /device:TPU:29 now
where the time goes in v2:
time: 75.7 us; the launch traced here: 75.6 us
  Pallas kernels  72.8 us (96%)
  local copies, waits for them, and re-layouts  2.21 us (3%)
    pallas_call x1, Pallas kernels, local_fn(): pl.pallas_call(body, out_shape=jax.ShapeDtypeStruct((TOK, DM), BF), in_sp...  72.8 us
    unnamed x1, local copies, waits for them, and re-layouts  2.21 us

profile of v2, /device:TPU:29, one launch (start us, length us, event | category | flops | bytes accessed | tf_op | source)
XLA Modules:
  0.0 75.6 jit_solution(959314668829608235)
XLA Ops:
  0.0 0.5 multiply_power_fusion.freq_ref
  0.5 72.8 %shard_map.55 = bf16[192,2560]{1,0:T(8,128)(2,1)} custom-call(f32[1,128]{1,0:T(1,128)} %multiply_power_fusion.freq_ref, bf16[192,2560]{1,0:T(8,128)(2,1)} %x_hbm.1, bf16[2560,8,256]{2,1,0:T(8,128)(2,1)} %wq_hbm.1, bf16[2560,4,256]{2,1,0:T(4,128)(2,1)} %wk_hbm.1, bf16[2560,4,256]{2,1,0:T(4,128)(2,1)} %wv_hbm.1, bf16[2048,2560]{1,0:T(8,128)(2,1)} %bitcast.1), custom_call_target="tpu_custom_call" | custom-call | tf_op jit(solution)/shard_map/pallas_call | solution.py:358
  73.4 2.2 %copy.7 = bf16[192,2560]{1,0:T(8,128)(2,1)} copy(bf16[192,2560]{1,0:T(8,128)(2,1)} %shard_map.55) | data formatting | bytes 1966080

commit v3 on v2

v3 whole, which is shorter than its diff:
```python
import jax
import jax.numpy as jnp
import numpy as np
from jax import lax
from jax.experimental import pallas as pl
from jax.experimental.pallas import tpu as pltpu
from jax.sharding import PartitionSpec as P

WINDOW = 2048
ROPE_BASE = 10000.0
MESH = pl.DeviceIdType.MESH
NL = 4
TOK = 192
LVL = NL * TOK
DM = 2560
HD = 256
HALF = HD // 2
NEG = -1e30
SCALE = HD ** -0.5 * 1.4426950408889634
KCUT = 2
QCUT = 4
OWN_KEYS = (256, 384, 640, 768)
F32, BF = jnp.float32, jnp.bfloat16


def body(trig_hbm, base_hbm, x_hbm, wq_hbm, wk_hbm, wv_hbm, wo_hbm, y_ref,
         trig, base, x, wq, wk, wv, wo, ko, vo, qo, kb, vb, qb, ob, osend, acc, m_s, l_s,
         tsem, xsem, wksem, wvsem, wqsem, wosem, krecv, vrecv, kfs, vfs, qfs, ksend, vsend, qsend, qrecv,
         os_sem, orecv, go):
    d, a, b = lax.axis_index("dp"), lax.axis_index("cpo"), lax.axis_index("cpi")
    shard = a * NL + b
    odd = lax.rem(b, 2)
    even = odd == 0
    partner = b + 1 - 2 * odd
    far = lax.rem(b + 2, NL)
    far2 = lax.rem(partner + 2, NL)
    near0 = b - odd
    away0 = 2 - near0
    donor = (a == 3) & even
    host = (a == 2) & even
    feeds = (a < 2) | ((a == 2) & (odd == 1))

    def cut(src, dst, sem, n, c):
        r = DM // n
        return pltpu.make_async_copy(src.at[pl.ds(c * r, r)], dst.at[pl.ds(c * r, r)], sem.at[c])

    xcopy = pltpu.make_async_copy(x_hbm, x, xsem)
    xcopy.start()
    for c in range(KCUT):
        cut(wk_hbm, wk, wksem, KCUT, c).start()
    trig_copy = pltpu.make_async_copy(trig_hbm, trig, tsem.at[0])
    base_copy = pltpu.make_async_copy(base_hbm, base, tsem.at[1])
    trig_copy.start()
    base_copy.start()
    for c in range(KCUT):
        cut(wv_hbm, wv, wvsem, KCUT, c).start()

    bar = pltpu.get_barrier_semaphore()

    def greet(level, other):
        pl.semaphore_signal(bar, inc=1, device_id=(d, level, other), device_id_type=MESH)

    for j in (partner, far, far2):
        greet(a, j)

    @pl.when(a > 0)
    def _():
        greet(a - 1, b)

    @pl.when(a < NL - 1)
    def _():
        greet(a + 1, b)

    @pl.when(host)
    def _():
        for j in (partner, far, far2):
            greet(3, j)

    @pl.when(a == 3)
    def _():
        greet(2, lax.rem(b + 2 - odd, NL))

    @pl.when((a == 3) & (odd == 1))
    def _():
        greet(2, b - 1)

    def one(p):
        return p.astype(jnp.int32)

    def project(w, n, copies, heads, between):
        total = None
        for c in range(n):
            copies[c].wait()
            r = DM // n
            part = jnp.dot(x[:, c * r:(c + 1) * r], w[pl.ds(c * r, r)].reshape(r, heads * HD),
                           preferred_element_type=F32)
            total = part if total is None else total + part
            if c in between:
                between[c]()
        return total

    def rotate(t, h, cos, sin):
        lo, hi = t[:, h * HD:h * HD + HALF], t[:, h * HD + HALF:(h + 1) * HD]
        return (lo * cos - hi * sin).astype(BF), (hi * cos + lo * sin).astype(BF)

    def rows(s):
        return pl.ds(pl.multiple_of(s * TOK, TOK), TOK)

    def remote(src, dst, ss, rs, dev):
        return pltpu.make_async_remote_copy(src_ref=src, dst_ref=dst, send_sem=ss, recv_sem=rs,
                                            device_id=dev, device_id_type=MESH)

    def exchange(h, what):
        dev = (d, a, h)
        if what == "k":
            return remote(ko.at[h], kb.at[rows(shard)], ksend.at[h], krecv.at[shard], dev)
        if what == "v":
            return remote(vo.at[h], vb.at[rows(shard)], vsend.at[h], vrecv.at[shard], dev)
        return remote(qo.at[h], qb.at[0, b], qsend.at[h], qrecv.at[0, b], dev)

    def send(what, heads):
        for h in heads:
            @pl.when(b != h)
            def _():
                exchange(h, what).start()

    def hop(s, what, level):
        dev = (d, level, b)
        if what == "k":
            return remote(kb.at[rows(s)], kb.at[rows(s)], kfs.at[s], krecv.at[s], dev)
        return remote(vb.at[rows(s)], vb.at[rows(s)], vfs.at[s], vrecv.at[s], dev)

    def wait_piece(s):
        hop(s, "k", a).wait_recv()
        hop(s, "v", a).wait_recv()

    def needed(s, level):
        return s >= NL * level - 11

    def pass_on(s, whats=("k", "v")):
        @pl.when(feeds & needed(s, a + 1))
        def _():
            for what in whats:
                hop(s, what, a + 1).start()

        @pl.when(donor)
        def _():
            for what in whats:
                hop(s, what, 2).start()

    def q_down(j):
        return remote(qb.at[0, j], qb.at[1, j], qfs.at[j], qrecv.at[1, j], (d, 2, b))

    def wait_q(slot, j):
        remote(qo.at[0], qb.at[slot, j], qsend.at[0], qrecv.at[slot, j], (d, a, b)).wait_recv()

    first_user = even | (a >= 2)

    xcopy.wait()
    with jax.named_scope("k_proj"):
        k_f = project(wk, KCUT, [cut(wk_hbm, wk, wksem, KCUT, c) for c in range(KCUT)], NL, {})
    for c in range(QCUT):
        cut(wq_hbm, wq, wqsem, QCUT, c).start()
    wo_copy = pltpu.make_async_copy(wo_hbm, wo, wosem)
    wo_copy.start()
    trig_copy.wait()
    base_copy.wait()
    cb, sb = base[0, pl.ds(shard, 1), :], base[1, pl.ds(shard, 1), :]
    cos = cb * trig[0] - sb * trig[1]
    sin = sb * trig[0] + cb * trig[1]
    for h in range(NL):
        ko[h, :, :HALF], ko[h, :, HALF:] = rotate(k_f, h, cos, sin)
    kb[rows(shard), :] = ko[b]
    with jax.named_scope("barrier"):
        pl.semaphore_wait(bar, 3 + one(a > 0) + one(a < NL - 1) + 3 * one(host) + one(a == 3)
                          + one((a == 3) & (odd == 1)))
    send("k", (0, 2))

    @pl.when(first_user)
    def _():
        pass_on(shard, ("k",))

    with jax.named_scope("v_proj"):
        v_f = project(wv, KCUT, [cut(wv_hbm, wv, wvsem, KCUT, c) for c in range(KCUT)], NL, {})
    for h in range(NL):
        vo[h] = v_f[:, h * HD:(h + 1) * HD].astype(BF)
    vb[rows(shard), :] = vo[b]
    send("v", (0, 2))

    @pl.when(first_user)
    def _():
        pass_on(shard, ("v",))

    def relay_partner():
        @pl.when(even)
        def _():
            wait_piece(a * NL + partner)
            pass_on(a * NL + partner)

    with jax.named_scope("q_proj"):
        q_f = project(wq, QCUT, [cut(wq_hbm, wq, wqsem, QCUT, c) for c in range(QCUT)], 2 * NL, {1: relay_partner})
    for h in range(2 * NL):
        qo[h // 2, h % 2, :, :HALF], qo[h // 2, h % 2, :, HALF:] = rotate(q_f, h, cos, sin)
    qb[0, b] = qo[b]
    send("q", (0, 2))
    send("k", (1, 3))
    send("v", (1, 3))
    send("q", (1, 3))

    def attend(slot, shards, level, key0, n, masked, first):
        keys = pl.ds(pl.multiple_of(key0, 64), n)
        k, v = kb[keys, :], vb[keys, :]
        chains = [(i, g) for i in shards for g in range(2)]
        scores = []
        for i, g in chains:
            s = lax.dot_general(qb[slot, i, g], k, (((1,), (1,)), ((), ())), preferred_element_type=F32)
            if masked:
                gap = (lax.broadcasted_iota(jnp.int32, (TOK, n), 0) - lax.broadcasted_iota(jnp.int32, (TOK, n), 1)
                       + (level * LVL + i * TOK - key0))
                s = jnp.where((gap >= 0) & (gap < WINDOW), s, NEG)
            scores.append(s)
        for (i, g), s in zip(chains, scores):
            top = jnp.max(s, axis=-1, keepdims=True)
            if first:
                new = top
            else:
                old = m_s[i, g]
                new = jnp.maximum(old, top)
                fix = jnp.exp2((old - new) * SCALE)
            p = jnp.exp2((s - new) * SCALE)
            total = jnp.sum(p, axis=-1, keepdims=True)
            out = jnp.dot(p.astype(BF), v, preferred_element_type=F32)
            if not first:
                total = total + l_s[i, g] * fix
                out = out + acc[i, g] * fix
            m_s[i, g] = new
            l_s[i, g] = total
            acc[i, g] = out

    def loop(lo, hi, fn):
        def step(i, carry):
            fn(i)
            return carry
        lax.fori_loop(lo, hi, step, 0)

    def head_cols():
        return pl.ds(pl.multiple_of(b * 2 * HD, 2 * HD), 2 * HD)

    def back_to(slot, i):
        return remote(osend.at[slot, i], ob.at[:, head_cols()], os_sem.at[slot, i], orecv.at[b], (d, a + slot, i))

    def finish(slot, i):
        for g in range(2):
            osend[slot, i, :, g * HD:(g + 1) * HD] = (acc[i, g] / l_s[i, g]).astype(BF)
        if slot == 1:
            back_to(1, i).start()
            return

        @pl.when(b != i)
        def _():
            back_to(0, i).start()

        @pl.when(b == i)
        def _():
            ob[:, head_cols()] = osend[0, i]

    def turn(t):
        return lax.rem(away0 + t, NL)

    low = (a - 1) * NL

    def own_block(slot):
        with jax.named_scope("own_att"):
            for i in range(NL):
                attend(slot, (i,), a + slot, (a + slot) * LVL, OWN_KEYS[i], True, True)

    def take(s):
        wait_piece(s)
        pass_on(s)

    @pl.when(even)
    def _():
        with jax.named_scope("own_pieces"):
            for j in (far, far2):
                take(a * NL + j)

    @pl.when((odd == 1) & (a >= 2))
    def _():
        with jax.named_scope("own_pieces"):
            for j in (partner, far, far2):
                take(a * NL + j)

    @pl.when(even & (a == 1))
    def _():
        with jax.named_scope("take_low"):
            for j in (b, partner, far, far2):
                take(low + j)
            for s in (shard, NL + partner, NL + far, NL + far2, b, partner):
                hop(s, "k", 2).wait_send()
                hop(s, "v", 2).wait_send()

    @pl.when(even & (a < 2))
    def _():
        pl.semaphore_signal(go, inc=1, device_id=(d, a, partner), device_id_type=MESH)

    @pl.when((odd == 1) & (a < 2))
    def _():
        with jax.named_scope("go_wait"):
            pl.semaphore_wait(go, 1)
        pass_on(shard)
        for j in (partner, far, far2):
            take(a * NL + j)

        @pl.when(a == 1)
        def _():
            with jax.named_scope("take_low"):
                for j in (b, partner, far, far2):
                    take(low + j)

    with jax.named_scope("own_q"):
        for j in (partner, far, far2):
            @pl.when(jnp.logical_not(donor))
            def _():
                wait_q(0, j)

    @pl.when(donor)
    def _():
        q_down(b).start()
        for j in (partner, far, far2):
            wait_q(0, j)
            q_down(j).start()

    @pl.when(jnp.logical_not(donor))
    def _():
        own_block(0)

        @pl.when(a == 0)
        def _():
            loop(0, NL, lambda t: finish(0, turn(t)))

        @pl.when(a > 0)
        def _():
            @pl.when(a >= 2)
            def _():
                with jax.named_scope("take1"):
                    for j in (b, partner, far, far2):
                        take(low + j)

            with jax.named_scope("att1"):
                loop(0, NL, lambda i: attend(0, (i,), a, (a - 1) * LVL, LVL, False, False))

            @pl.when(a == 1)
            def _():
                loop(0, NL, lambda t: finish(0, turn(t)))

        @pl.when(host)
        def _():
            with jax.named_scope("take2"):
                for j in (b, partner, far, far2):
                    take(j)

            def last(t):
                attend(0, (turn(t),), a, 0, LVL, True, False)
                finish(0, turn(t))
            with jax.named_scope("att2"):
                loop(0, NL, last)

        @pl.when((a >= 2) & (odd == 1))
        def _():
            lvl2 = (a - 2) * NL
            with jax.named_scope("take2a"):
                for j in (b, partner):
                    take(lvl2 + j)
            with jax.named_scope("att2a"):
                loop(0, 2, lambda t: attend(0, (2 * t, 2 * t + 1), a, (lvl2 + near0) * TOK, 2 * TOK, True, False))
            with jax.named_scope("take2b"):
                for j in (far, far2):
                    take(lvl2 + j)

            def last(t):
                i = turn(2 * t)
                attend(0, (i, i + 1), a, (lvl2 + away0) * TOK, 2 * TOK, True, False)

                @pl.when(a == 2)
                def _():
                    finish(0, i)
                    finish(0, i + 1)
            with jax.named_scope("att2b"):
                loop(0, 2, last)

        @pl.when((a == 3) & (odd == 1))
        def _():
            finish(0, NL - 1)
            with jax.named_scope("take3"):
                for j in (b, partner, far, far2):
                    @pl.when(j > 0)
                    def _():
                        wait_piece(j)

            def last(t):
                @pl.when(turn(t) < NL - 1)
                def _():
                    attend(0, (turn(t),), a, 256, 512, True, False)
                    finish(0, turn(t))
            with jax.named_scope("att3"):
                loop(0, NL, last)

    @pl.when(host)
    def _():
        with jax.named_scope("host_wait"):
            for j in range(NL):
                wait_piece(3 * NL + j)
            for j in range(NL):
                wait_q(1, j)
        own_block(1)

        def each(i):
            attend(1, (i,), 3, 2 * LVL, LVL, False, False)
            attend(1, (i,), 3, LVL, LVL, True, False)

            @pl.when(i < NL - 1)
            def _():
                attend(1, (i,), 3, 256, 512, True, False)
            finish(1, i)
        with jax.named_scope("host_att"):
            loop(0, NL, each)

    def take_o(h):
        @pl.when((b != h) | ((a == 3) & (h % 2 == 0)))
        def _():
            remote(osend.at[0, 0], ob.at[:, pl.ds(h * 2 * HD, 2 * HD)], os_sem.at[0, 0], orecv.at[h], (d, a, b)).wait_recv()

    def project_o(h):
        return jnp.dot(ob[:, h * 2 * HD:(h + 1) * 2 * HD], wo[pl.ds(h * 2 * HD, 2 * HD), :],
                       preferred_element_type=F32)

    with jax.named_scope("o_even"):
        take_o(0)
        take_o(2)
    wo_copy.wait()
    y = project_o(0) + project_o(2)
    with jax.named_scope("o_odd"):
        take_o(1)
        take_o(3)
    y_ref[...] = (y + project_o(1) + project_o(3)).astype(BF)

    for h in range(NL):
        @pl.when(b != h)
        def _():
            for what in ("k", "v", "q"):
                exchange(h, what).wait_send()

        @pl.when((b != h) & jnp.logical_not(donor))
        def _():
            back_to(0, h).wait_send()

        @pl.when(host)
        def _():
            back_to(1, h).wait_send()

        @pl.when(donor)
        def _():
            q_down(h).wait_send()
            for what in ("k", "v"):
                hop(3 * NL + h, what, 2).wait_send()

    for s in range(12):
        waited = even & (a == 1) & ((s >= NL) | (s // 2 == b // 2))

        @pl.when(feeds & (s < NL * (a + 1)) & needed(s, a + 1) & jnp.logical_not(waited))
        def _():
            for what in ("k", "v"):
                hop(s, what, a + 1).wait_send()


def solution(mesh):
    def local_fn(hidden, w_q, w_k, w_v, w_o):
        freq = ROPE_BASE ** (-np.arange(HALF) * 2.0 / HD)
        steps, starts = np.arange(TOK)[:, None] * freq, (np.arange(NL * NL) * TOK)[:, None] * freq
        trig = jnp.asarray(np.stack([np.cos(steps), np.sin(steps)]), F32)
        base = jnp.asarray(np.stack([np.cos(starts), np.sin(starts)]), F32)
        vm, hbm = pl.BlockSpec(memory_space=pltpu.VMEM), pl.BlockSpec(memory_space=pl.ANY)
        dma = pltpu.SemaphoreType.DMA
        return pl.pallas_call(
            body,
            out_shape=jax.ShapeDtypeStruct((TOK, DM), BF),
            in_specs=[hbm] * 7,
            out_specs=vm,
            scratch_shapes=[
                pltpu.VMEM((2, TOK, HALF), F32), pltpu.VMEM((2, NL * NL, HALF), F32),
                pltpu.VMEM((TOK, DM), BF), pltpu.VMEM((DM, 2 * NL, HD), BF), pltpu.VMEM((DM, NL, HD), BF),
                pltpu.VMEM((DM, NL, HD), BF), pltpu.VMEM((2 * NL * HD, DM), BF),
                pltpu.VMEM((NL, TOK, HD), BF), pltpu.VMEM((NL, TOK, HD), BF), pltpu.VMEM((NL, 2, TOK, HD), BF),
                pltpu.VMEM((16 * TOK, HD), BF), pltpu.VMEM((16 * TOK, HD), BF),
                pltpu.VMEM((2, NL, 2, TOK, HD), BF), pltpu.VMEM((TOK, 2 * NL * HD), BF),
                pltpu.VMEM((2, NL, TOK, 2 * HD), BF), pltpu.VMEM((NL, 2, TOK, HD), F32),
                pltpu.VMEM((NL, 2, TOK, 1), F32), pltpu.VMEM((NL, 2, TOK, 1), F32),
                dma((2,)), dma(()), dma((KCUT,)), dma((KCUT,)), dma((QCUT,)), dma(()),
                dma((16,)), dma((16,)), dma((16,)), dma((16,)), dma((NL,)),
                dma((NL,)), dma((NL,)), dma((NL,)), dma((2, NL)), dma((2, NL)), dma((NL,)),
                pltpu.SemaphoreType.REGULAR,
            ],
            compiler_params=pltpu.CompilerParams(collective_id=0, has_side_effects=True,
                                                 vmem_limit_bytes=63 * 2 ** 20),
        )(trig, base, hidden, w_q, w_k, w_v, w_o.reshape(2 * NL * HD, DM))

    return jax.shard_map(local_fn, mesh=mesh,
                         in_specs=(P(("dp", "cpo", "cpi"), None), P(), P(), P(), P()),
                         out_specs=P(("dp", "cpo", "cpi"), None), check_vma=False)
```

time: 75.7 us -> 65 us (0.86)
  the two profiles are of different devices: /device:TPU:29 before, /device:TPU:27 now
where the time goes in v3:
time: 65 us; the launch traced here: 64.9 us
  Pallas kernels  62.7 us (96%)
  local copies, waits for them, and re-layouts  2.21 us (3%)
    pallas_call x1, Pallas kernels, local_fn(): pl.pallas_call(body, out_shape=jax.ShapeDtypeStruct((TOK, DM), BF), in_sp...  62.7 us
    unnamed x1, local copies, waits for them, and re-layouts  2.21 us

profile of v3, /device:TPU:27, one launch (start us, length us, event | category | flops | bytes accessed | tf_op | source)
XLA Modules:
  0.0 64.9 jit_solution(7607566416468159602)
XLA Ops:
  0.0 62.7 %shard_map.73 = bf16[192,2560]{1,0:T(8,128)(2,1)} custom-call(f32[2,192,128]{2,1,0:T(8,128)} %constant.4.clone.trig_hbm, f32[2,16,128]{2,1,0:T(8,128)} %constant.5.clone.base_hbm, bf16[192,2560]{1,0:T(8,128)(2,1)} %x_hbm.1, bf16[2560,8,256]{2,1,0:T(8,128)(2,1)} %wq_hbm.1, bf16[2560,4,256]{2,1,0:T(4,128)(2,1)} %wk_hbm.1, bf16[2560,4,256]{2,1,0:T(4,128)(2,1)} %wv_hbm.1, ...), custom_call_target="tpu_custom_call" | custom-call | tf_op jit(solution)/shard_map/pallas_call | solution.py:484
  62.7 2.2 %copy.9 = bf16[192,2560]{1,0:T(8,128)(2,1)} copy(bf16[192,2560]{1,0:T(8,128)(2,1)} %shard_map.73) | data formatting | bytes 1966080

commit v4 on v3

--- a/solution.py
+++ b/solution.py
@@ -15,6 +15,8 @@
 DM = 2560
 HD = 256
 HALF = HD // 2
+LANES = 128
+YCOLS = 512
 NEG = -1e30
 SCALE = HD ** -0.5 * 1.4426950408889634
 KCUT = 2
@@ -24,9 +26,9 @@
 
 
 def body(trig_hbm, base_hbm, x_hbm, wq_hbm, wk_hbm, wv_hbm, wo_hbm, y_ref,
-         trig, base, x, wq, wk, wv, wo, ko, vo, qo, kb, vb, qb, ob, osend, acc, m_s, l_s,
+         trig, base, x, wq, wk, wv, wo, ko, vo, qo, kb, vb, qb, ob, osend, acc, m_s, l_s, y_acc, y_tile,
          tsem, xsem, wksem, wvsem, wqsem, wosem, krecv, vrecv, kfs, vfs, qfs, ksend, vsend, qsend, qrecv,
-         os_sem, orecv, go):
+         os_sem, orecv, ysem, go):
     d, a, b = lax.axis_index("dp"), lax.axis_index("cpo"), lax.axis_index("cpi")
     shard = a * NL + b
     odd = lax.rem(b, 2)
@@ -46,14 +48,9 @@
 
     xcopy = pltpu.make_async_copy(x_hbm, x, xsem)
     xcopy.start()
-    for c in range(KCUT):
-        cut(wk_hbm, wk, wksem, KCUT, c).start()
+    cut(wk_hbm, wk, wksem, KCUT, 0).start()
     trig_copy = pltpu.make_async_copy(trig_hbm, trig, tsem.at[0])
     base_copy = pltpu.make_async_copy(base_hbm, base, tsem.at[1])
-    trig_copy.start()
-    base_copy.start()
-    for c in range(KCUT):
-        cut(wv_hbm, wv, wvsem, KCUT, c).start()
 
     bar = pltpu.get_barrier_semaphore()
 
@@ -157,6 +154,12 @@
     first_user = even | (a >= 2)
 
     xcopy.wait()
+    for c in range(1, KCUT):
+        cut(wk_hbm, wk, wksem, KCUT, c).start()
+    trig_copy.start()
+    base_copy.start()
+    for c in range(KCUT):
+        cut(wv_hbm, wv, wvsem, KCUT, c).start()
     with jax.named_scope("k_proj"):
         k_f = project(wk, KCUT, [cut(wk_hbm, wk, wksem, KCUT, c) for c in range(KCUT)], NL, {})
     for c in range(QCUT):
@@ -174,7 +177,7 @@
     with jax.named_scope("barrier"):
         pl.semaphore_wait(bar, 3 + one(a > 0) + one(a < NL - 1) + 3 * one(host) + one(a == 3)
                           + one((a == 3) & (odd == 1)))
-    send("k", (0, 2))
+    send("k", (0, 2, 1, 3))
 
     @pl.when(first_user)
     def _():
@@ -185,7 +188,7 @@
     for h in range(NL):
         vo[h] = v_f[:, h * HD:(h + 1) * HD].astype(BF)
     vb[rows(shard), :] = vo[b]
-    send("v", (0, 2))
+    send("v", (0, 2, 1, 3))
 
     @pl.when(first_user)
     def _():
@@ -202,40 +205,44 @@
     for h in range(2 * NL):
         qo[h // 2, h % 2, :, :HALF], qo[h // 2, h % 2, :, HALF:] = rotate(q_f, h, cos, sin)
     qb[0, b] = qo[b]
-    send("q", (0, 2))
-    send("k", (1, 3))
-    send("v", (1, 3))
-    send("q", (1, 3))
-
-    def attend(slot, shards, level, key0, n, masked, first):
+    send("q", (0, 2, 1, 3))
+
+    def wide(t, n):
+        return jnp.concatenate([t] * (n // LANES), axis=1)
+
+    def attend(slot, i, level, key0, n, masked, first=False, last=False):
         keys = pl.ds(pl.multiple_of(key0, 64), n)
         k, v = kb[keys, :], vb[keys, :]
-        chains = [(i, g) for i in shards for g in range(2)]
         scores = []
-        for i, g in chains:
+        for g in range(2):
             s = lax.dot_general(qb[slot, i, g], k, (((1,), (1,)), ((), ())), preferred_element_type=F32)
             if masked:
                 gap = (lax.broadcasted_iota(jnp.int32, (TOK, n), 0) - lax.broadcasted_iota(jnp.int32, (TOK, n), 1)
                        + (level * LVL + i * TOK - key0))
                 s = jnp.where((gap >= 0) & (gap < WINDOW), s, NEG)
             scores.append(s)
-        for (i, g), s in zip(chains, scores):
+        for g, s in enumerate(scores):
             top = jnp.max(s, axis=-1, keepdims=True)
             if first:
-                new = top
+                new = jnp.broadcast_to(top, (TOK, LANES))
             else:
                 old = m_s[i, g]
                 new = jnp.maximum(old, top)
                 fix = jnp.exp2((old - new) * SCALE)
-            p = jnp.exp2((s - new) * SCALE)
-            total = jnp.sum(p, axis=-1, keepdims=True)
+            p = jnp.exp2((s - wide(new, n)) * SCALE)
+            total = jnp.broadcast_to(jnp.sum(p, axis=-1, keepdims=True), (TOK, LANES))
             out = jnp.dot(p.astype(BF), v, preferred_element_type=F32)
             if not first:
                 total = total + l_s[i, g] * fix
-                out = out + acc[i, g] * fix
-            m_s[i, g] = new
-            l_s[i, g] = total
-            acc[i, g] = out
+                out = out + acc[i, g] * wide(fix, HD)
+            if last:
+                osend[slot, i, :, g * HD:(g + 1) * HD] = (out * wide(1.0 / total, HD)).astype(BF)
+            else:
+                m_s[i, g] = new
+                l_s[i, g] = total
+                acc[i, g] = out
+        if last:
+            give(slot, i)
 
     def loop(lo, hi, fn):
         def step(i, carry):
@@ -249,9 +256,7 @@
     def back_to(slot, i):
         return remote(osend.at[slot, i], ob.at[:, head_cols()], os_sem.at[slot, i], orecv.at[b], (d, a + slot, i))
 
-    def finish(slot, i):
-        for g in range(2):
-            osend[slot, i, :, g * HD:(g + 1) * HD] = (acc[i, g] / l_s[i, g]).astype(BF)
+    def give(slot, i):
         if slot == 1:
             back_to(1, i).start()
             return
@@ -264,6 +269,11 @@
         def _():
             ob[:, head_cols()] = osend[0, i]
 
+    def finish(slot, i):
+        for g in range(2):
+            osend[slot, i, :, g * HD:(g + 1) * HD] = (acc[i, g] * wide(1.0 / l_s[i, g], HD)).astype(BF)
+        give(slot, i)
+
     def turn(t):
         return lax.rem(away0 + t, NL)
 
@@ -272,7 +282,7 @@
     def own_block(slot):
         with jax.named_scope("own_att"):
             for i in range(NL):
-                attend(slot, (i,), a + slot, (a + slot) * LVL, OWN_KEYS[i], True, True)
+                attend(slot, i, a + slot, (a + slot) * LVL, OWN_KEYS[i], True, first=True)
 
     def take(s):
         wait_piece(s)
@@ -314,7 +324,7 @@
         @pl.when(a == 1)
         def _():
             with jax.named_scope("take_low"):
-                for j in (b, partner, far, far2):
+                for j in (3, 2, 1, 0):
                     take(low + j)
 
     with jax.named_scope("own_q"):
@@ -346,64 +356,59 @@
                     for j in (b, partner, far, far2):
                         take(low + j)
 
-            with jax.named_scope("att1"):
-                loop(0, NL, lambda i: attend(0, (i,), a, (a - 1) * LVL, LVL, False, False))
-
             @pl.when(a == 1)
             def _():
-                loop(0, NL, lambda t: finish(0, turn(t)))
+                loop(0, NL, lambda t: attend(0, turn(t), a, 0, LVL, False, last=True))
+
+            @pl.when(a > 1)
+            def _():
+                with jax.named_scope("att1"):
+                    loop(0, NL, lambda i: attend(0, i, a, (a - 1) * LVL, LVL, False))
 
         @pl.when(host)
         def _():
             with jax.named_scope("take2"):
                 for j in (b, partner, far, far2):
                     take(j)
-
-            def last(t):
-                attend(0, (turn(t),), a, 0, LVL, True, False)
-                finish(0, turn(t))
             with jax.named_scope("att2"):
-                loop(0, NL, last)
+                loop(0, NL, lambda t: attend(0, turn(t), a, 0, LVL, True, last=True))
 
         @pl.when((a >= 2) & (odd == 1))
         def _():
             lvl2 = (a - 2) * NL
             with jax.named_scope("take2a"):
-                for j in (b, partner):
-                    take(lvl2 + j)
+                take(lvl2 + 3)
+                take(lvl2 + 2)
             with jax.named_scope("att2a"):
-                loop(0, 2, lambda t: attend(0, (2 * t, 2 * t + 1), a, (lvl2 + near0) * TOK, 2 * TOK, True, False))
+                loop(0, 2, lambda i: attend(0, i, a, lvl2 * TOK + 2 * TOK, 2 * TOK, False))
             with jax.named_scope("take2b"):
-                for j in (far, far2):
-                    take(lvl2 + j)
-
-            def last(t):
-                i = turn(2 * t)
-                attend(0, (i, i + 1), a, (lvl2 + away0) * TOK, 2 * TOK, True, False)
-
-                @pl.when(a == 2)
-                def _():
-                    finish(0, i)
-                    finish(0, i + 1)
+                take(lvl2 + 1)
             with jax.named_scope("att2b"):
-                loop(0, 2, last)
+                loop(2, NL, lambda i: attend(0, i, a, lvl2 * TOK + 2 * TOK, 2 * TOK, False))
+            with jax.named_scope("take2c"):
+                take(lvl2)
+
+        @pl.when((a == 2) & (odd == 1))
+        def _():
+            with jax.named_scope("att2c"):
+                loop(0, NL, lambda t: attend(0, turn(t), a, 0, 2 * TOK, True, last=True))
 
         @pl.when((a == 3) & (odd == 1))
         def _():
+            with jax.named_scope("att2c"):
+                loop(0, NL, lambda i: attend(0, i, a, LVL, 2 * TOK, True))
             finish(0, NL - 1)
             with jax.named_scope("take3"):
-                for j in (b, partner, far, far2):
-                    @pl.when(j > 0)
-                    def _():
-                        wait_piece(j)
-
-            def last(t):
-                @pl.when(turn(t) < NL - 1)
-                def _():
-                    attend(0, (turn(t),), a, 256, 512, True, False)
-                    finish(0, turn(t))
+                wait_piece(3)
+                wait_piece(2)
             with jax.named_scope("att3"):
-                loop(0, NL, last)
+                attend(0, 2, a, 2 * TOK, 2 * TOK, True, last=True)
+                attend(0, 1, a, 2 * TOK, 2 * TOK, True, last=True)
+                attend(0, 0, a, 2 * TOK, 2 * TOK, True)
+            with jax.named_scope("take3b"):
+                wait_piece(1)
+            with jax.named_scope("att3b"):
+                attend(0, 0, a, 256, 128, True, last=True)
 
     @pl.when(host)
     def _():
@@ -415,13 +420,12 @@
         own_block(1)
 
         def each(i):
-            attend(1, (i,), 3, 2 * LVL, LVL, False, False)
-            attend(1, (i,), 3, LVL, LVL, True, False)
+            attend(1, i, 3, 2 * LVL, LVL, False)
 
             @pl.when(i < NL - 1)
             def _():
-                attend(1, (i,), 3, 256, 512, True, False)
-            finish(1, i)
+                attend(1, i, 3, 256, 512, True)
+            attend(1, i, 3, LVL, LVL, True, last=True)
         with jax.named_scope("host_att"):
             loop(0, NL, each)
 
@@ -430,19 +434,26 @@
         def _():
             remote(osend.at[0, 0], ob.at[:, pl.ds(h * 2 * HD, 2 * HD)], os_sem.at[0, 0], orecv.at[h], (d, a, b)).wait_recv()
 
-    def project_o(h):
-        return jnp.dot(ob[:, h * 2 * HD:(h + 1) * 2 * HD], wo[pl.ds(h * 2 * HD, 2 * HD), :],
+    def project_o(h, cols):
+        return jnp.dot(ob[:, h * 2 * HD:(h + 1) * 2 * HD], wo[pl.ds(h * 2 * HD, 2 * HD), cols],
                        preferred_element_type=F32)
 
+    tiles = [pl.ds(t * YCOLS, YCOLS) for t in range(DM // YCOLS)]
     with jax.named_scope("o_even"):
         take_o(0)
         take_o(2)
     wo_copy.wait()
-    y = project_o(0) + project_o(2)
+    for cols in tiles:
+        y_acc[:, cols] = project_o(0, cols) + project_o(2, cols)
     with jax.named_scope("o_odd"):
         take_o(1)
         take_o(3)
-    y_ref[...] = (y + project_o(1) + project_o(3)).astype(BF)
+    y_copies = []
+    with jax.named_scope("y_out"):
+        for t, cols in enumerate(tiles):
+            y_tile[:, cols] = (y_acc[:, cols] + project_o(1, cols) + project_o(3, cols)).astype(BF)
+            y_copies.append(pltpu.make_async_copy(y_tile.at[:, cols], y_ref.at[:, cols], ysem.at[t]))
+            y_copies[-1].start()
 
     for h in range(NL):
         @pl.when(b != h)
@@ -471,6 +482,8 @@
         def _():
             for what in ("k", "v"):
                 hop(s, what, a + 1).wait_send()
+    for c in y_copies:
+        c.wait()
 
 
 def solution(mesh):
@@ -479,13 +492,13 @@
         steps, starts = np.arange(TOK)[:, None] * freq, (np.arange(NL * NL) * TOK)[:, None] * freq
         trig = jnp.asarray(np.stack([np.cos(steps), np.sin(steps)]), F32)
         base = jnp.asarray(np.stack([np.cos(starts), np.sin(starts)]), F32)
-        vm, hbm = pl.BlockSpec(memory_space=pltpu.VMEM), pl.BlockSpec(memory_space=pl.ANY)
+        hbm = pl.BlockSpec(memory_space=pl.ANY)
         dma = pltpu.SemaphoreType.DMA
         return pl.pallas_call(
             body,
             out_shape=jax.ShapeDtypeStruct((TOK, DM), BF),
             in_specs=[hbm] * 7,
-            out_specs=vm,
+            out_specs=hbm,
             scratch_shapes=[
                 pltpu.VMEM((2, TOK, HALF), F32), pltpu.VMEM((2, NL * NL, HALF), F32),
                 pltpu.VMEM((TOK, DM), BF), pltpu.VMEM((DM, 2 * NL, HD), BF), pltpu.VMEM((DM, NL, HD), BF),
@@ -494,10 +507,11 @@
                 pltpu.VMEM((16 * TOK, HD), BF), pltpu.VMEM((16 * TOK, HD), BF),
                 pltpu.VMEM((2, NL, 2, TOK, HD), BF), pltpu.VMEM((TOK, 2 * NL * HD), BF),
                 pltpu.VMEM((2, NL, TOK, 2 * HD), BF), pltpu.VMEM((NL, 2, TOK, HD), F32),
-                pltpu.VMEM((NL, 2, TOK, 1), F32), pltpu.VMEM((NL, 2, TOK, 1), F32),
+                pltpu.VMEM((NL, 2, TOK, LANES), F32), pltpu.VMEM((NL, 2, TOK, LANES), F32),
+                pltpu.VMEM((TOK, DM), F32), pltpu.VMEM((TOK, DM), BF),
                 dma((2,)), dma(()), dma((KCUT,)), dma((KCUT,)), dma((QCUT,)), dma(()),
                 dma((16,)), dma((16,)), dma((16,)), dma((16,)), dma((NL,)),
-                dma((NL,)), dma((NL,)), dma((NL,)), dma((2, NL)), dma((2, NL)), dma((NL,)),
+                dma((NL,)), dma((NL,)), dma((NL,)), dma((2, NL)), dma((2, NL)), dma((NL,)), dma((DM // YCOLS,)),
                 pltpu.SemaphoreType.REGULAR,
             ],
             compiler_params=pltpu.CompilerParams(collective_id=0, has_side_effects=True,

time: 65 us -> 64.9 us (level)
  the two profiles are of different devices: /device:TPU:27 before, /device:TPU:26 now
where the time goes in v4:
time: 64.9 us; the launch traced here: 64.8 us
  Pallas kernels  62.6 us (96%)
  local copies, waits for them, and re-layouts  2.21 us (3%)
    pallas_call x1, Pallas kernels, local_fn(): pl.pallas_call(body, out_shape=jax.ShapeDtypeStruct((TOK, DM), BF), in_sp...  62.6 us
    unnamed x1, local copies, waits for them, and re-layouts  2.21 us

profile of v4, /device:TPU:26, one launch (start us, length us, event | category | flops | bytes accessed | tf_op | source)
XLA Modules:
  0.0 64.8 jit_solution(4162030422722033250)
XLA Ops:
  0.0 62.6 %shard_map.73 = bf16[192,2560]{1,0:T(8,128)(2,1)} custom-call(f32[2,192,128]{2,1,0:T(8,128)} %constant.4.clone.trig_hbm, f32[2,16,128]{2,1,0:T(8,128)} %constant.5.clone.base_hbm, bf16[192,2560]{1,0:T(8,128)(2,1)} %x_hbm.1, bf16[2560,8,256]{2,1,0:T(8,128)(2,1)} %wq_hbm.1, bf16[2560,4,256]{2,1,0:T(4,128)(2,1)} %wk_hbm.1, bf16[2560,4,256]{2,1,0:T(4,128)(2,1)} %wv_hbm.1, ...), custom_call_target="tpu_custom_call" | custom-call | tf_op jit(solution)/shard_map/pallas_call | solution.py:497
  62.6 2.2 %copy.9 = bf16[192,2560]{1,0:T(8,128)(2,1)} copy(bf16[192,2560]{1,0:T(8,128)(2,1)} %shard_map.73) | data formatting | bytes 1966080

commit v5 on v4

--- a/solution.py
+++ b/solution.py
@@ -19,7 +19,7 @@
 YCOLS = 512
 NEG = -1e30
 SCALE = HD ** -0.5 * 1.4426950408889634
-KCUT = 2
+KCUT = 4
 QCUT = 4
 OWN_KEYS = (256, 384, 640, 768)
 F32, BF = jnp.float32, jnp.bfloat16
@@ -48,7 +48,8 @@
 
     xcopy = pltpu.make_async_copy(x_hbm, x, xsem)
     xcopy.start()
-    cut(wk_hbm, wk, wksem, KCUT, 0).start()
+    for c in range(KCUT):
+        cut(wk_hbm, wk, wksem, KCUT, c).start()
     trig_copy = pltpu.make_async_copy(trig_hbm, trig, tsem.at[0])
     base_copy = pltpu.make_async_copy(base_hbm, base, tsem.at[1])
 
@@ -84,10 +85,12 @@
     def one(p):
         return p.astype(jnp.int32)
 
-    def project(w, n, copies, heads, between):
+    def project(w, n, copies, heads, fetch, between):
         total = None
         for c in range(n):
             copies[c].wait()
+            if c in fetch:
+                fetch[c]()
             r = DM // n
             part = jnp.dot(x[:, c * r:(c + 1) * r], w[pl.ds(c * r, r)].reshape(r, heads * HD),
                            preferred_element_type=F32)
@@ -151,21 +154,23 @@
     def wait_q(slot, j):
         remote(qo.at[0], qb.at[slot, j], qsend.at[0], qrecv.at[slot, j], (d, a, b)).wait_recv()
 
-    first_user = even | (a >= 2)
+    first_user = even | (a >= 1)
 
     xcopy.wait()
-    for c in range(1, KCUT):
-        cut(wk_hbm, wk, wksem, KCUT, c).start()
-    trig_copy.start()
-    base_copy.start()
-    for c in range(KCUT):
-        cut(wv_hbm, wv, wvsem, KCUT, c).start()
+
+    def start_v():
+        trig_copy.start()
+        base_copy.start()
+        for c in range(KCUT):
+            cut(wv_hbm, wv, wvsem, KCUT, c).start()
+
+    def start_q():
+        for c in range(QCUT):
+            cut(wq_hbm, wq, wqsem, QCUT, c).start()
+
     with jax.named_scope("k_proj"):
-        k_f = project(wk, KCUT, [cut(wk_hbm, wk, wksem, KCUT, c) for c in range(KCUT)], NL, {})
-    for c in range(QCUT):
-        cut(wq_hbm, wq, wqsem, QCUT, c).start()
+        k_f = project(wk, KCUT, [cut(wk_hbm, wk, wksem, KCUT, c) for c in range(KCUT)], NL, {1: start_v}, {})
     wo_copy = pltpu.make_async_copy(wo_hbm, wo, wosem)
-    wo_copy.start()
     trig_copy.wait()
     base_copy.wait()
     cb, sb = base[0, pl.ds(shard, 1), :], base[1, pl.ds(shard, 1), :]
@@ -177,31 +182,42 @@
     with jax.named_scope("barrier"):
         pl.semaphore_wait(bar, 3 + one(a > 0) + one(a < NL - 1) + 3 * one(host) + one(a == 3)
                           + one((a == 3) & (odd == 1)))
-    send("k", (0, 2, 1, 3))
+    send("k", (0, 2))
+
+    def relay(who, whats, js):
+        @pl.when(who)
+        def _():
+            for j in js:
+                for what in whats:
+                    hop(a * NL + j, what, a).wait_recv()
+                pass_on(a * NL + j, whats)
 
     @pl.when(first_user)
     def _():
         pass_on(shard, ("k",))
 
     with jax.named_scope("v_proj"):
-        v_f = project(wv, KCUT, [cut(wv_hbm, wv, wvsem, KCUT, c) for c in range(KCUT)], NL, {})
+        v_f = project(wv, KCUT, [cut(wv_hbm, wv, wvsem, KCUT, c) for c in range(KCUT)], NL, {1: start_q},
+                      {2: lambda: relay(even, ("k",), (partner,))})
     for h in range(NL):
         vo[h] = v_f[:, h * HD:(h + 1) * HD].astype(BF)
     vb[rows(shard), :] = vo[b]
-    send("v", (0, 2, 1, 3))
+    send("v", (0, 2))
+    send("k", (1, 3))
+    send("v", (1, 3))
 
     @pl.when(first_user)
     def _():
         pass_on(shard, ("v",))
 
-    def relay_partner():
-        @pl.when(even)
-        def _():
-            wait_piece(a * NL + partner)
-            pass_on(a * NL + partner)
+    def relay_1():
+        relay(even, ("v",), (partner,))
+        relay(even, ("k",), (far, far2))
+        relay((odd == 1) & (a >= 1), ("k", "v"), (partner,))
 
     with jax.named_scope("q_proj"):
-        q_f = project(wq, QCUT, [cut(wq_hbm, wq, wqsem, QCUT, c) for c in range(QCUT)], 2 * NL, {1: relay_partner})
+        q_f = project(wq, QCUT, [cut(wq_hbm, wq, wqsem, QCUT, c) for c in range(QCUT)], 2 * NL,
+                      {1: wo_copy.start}, {1: relay_1})
     for h in range(2 * NL):
         qo[h // 2, h % 2, :, :HALF], qo[h // 2, h % 2, :, HALF:] = rotate(q_f, h, cos, sin)
     qb[0, b] = qo[b]
@@ -226,21 +242,21 @@
             if first:
                 new = jnp.broadcast_to(top, (TOK, LANES))
             else:
-                old = m_s[i, g]
+                old = m_s[slot, i, g]
                 new = jnp.maximum(old, top)
                 fix = jnp.exp2((old - new) * SCALE)
             p = jnp.exp2((s - wide(new, n)) * SCALE)
             total = jnp.broadcast_to(jnp.sum(p, axis=-1, keepdims=True), (TOK, LANES))
             out = jnp.dot(p.astype(BF), v, preferred_element_type=F32)
             if not first:
-                total = total + l_s[i, g] * fix
-                out = out + acc[i, g] * wide(fix, HD)
+                total = total + l_s[slot, i, g] * fix
+                out = out + acc[slot, i, g] * wide(fix, HD)
             if last:
                 osend[slot, i, :, g * HD:(g + 1) * HD] = (out * wide(1.0 / total, HD)).astype(BF)
             else:
-                m_s[i, g] = new
-                l_s[i, g] = total
-                acc[i, g] = out
+                m_s[slot, i, g] = new
+                l_s[slot, i, g] = total
+                acc[slot, i, g] = out
         if last:
             give(slot, i)
 
@@ -271,7 +287,7 @@
 
     def finish(slot, i):
         for g in range(2):
-            osend[slot, i, :, g * HD:(g + 1) * HD] = (acc[i, g] * wide(1.0 / l_s[i, g], HD)).astype(BF)
+            osend[slot, i, :, g * HD:(g + 1) * HD] = (acc[slot, i, g] * wide(1.0 / l_s[slot, i, g], HD)).astype(BF)
         give(slot, i)
 
     def turn(t):
@@ -288,44 +304,26 @@
         wait_piece(s)
         pass_on(s)
 
-    @pl.when(even)
-    def _():
-        with jax.named_scope("own_pieces"):
-            for j in (far, far2):
-                take(a * NL + j)
-
-    @pl.when((odd == 1) & (a >= 2))
-    def _():
-        with jax.named_scope("own_pieces"):
-            for j in (partner, far, far2):
-                take(a * NL + j)
-
-    @pl.when(even & (a == 1))
+    relay(even, ("v",), (far, far2))
+
+    @pl.when(even & (a == 0))
+    def _():
+        pl.semaphore_signal(go, inc=1, device_id=(d, a, partner), device_id_type=MESH)
+
+    @pl.when((odd == 1) & (a == 0))
+    def _():
+        with jax.named_scope("go_wait"):
+            pl.semaphore_wait(go, 1)
+        pass_on(shard)
+        take(a * NL + partner)
+
+    relay(odd == 1, ("k", "v"), (far, far2))
+
+    @pl.when((even & (a == 1)) | ((odd == 1) & (a >= 2)))
     def _():
         with jax.named_scope("take_low"):
             for j in (b, partner, far, far2):
                 take(low + j)
-            for s in (shard, NL + partner, NL + far, NL + far2, b, partner):
-                hop(s, "k", 2).wait_send()
-                hop(s, "v", 2).wait_send()
-
-    @pl.when(even & (a < 2))
-    def _():
-        pl.semaphore_signal(go, inc=1, device_id=(d, a, partner), device_id_type=MESH)
-
-    @pl.when((odd == 1) & (a < 2))
-    def _():
-        with jax.named_scope("go_wait"):
-            pl.semaphore_wait(go, 1)
-        pass_on(shard)
-        for j in (partner, far, far2):
-            take(a * NL + j)
-
-        @pl.when(a == 1)
-        def _():
-            with jax.named_scope("take_low"):
-                for j in (3, 2, 1, 0):
-                    take(low + j)
 
     with jax.named_scope("own_q"):
         for j in (partner, far, far2):
@@ -350,15 +348,30 @@
 
         @pl.when(a > 0)
         def _():
-            @pl.when(a >= 2)
+            @pl.when(host)
             def _():
                 with jax.named_scope("take1"):
                     for j in (b, partner, far, far2):
                         take(low + j)
 
+            @pl.when((a == 1) & (odd == 1))
+            def _():
+                with jax.named_scope("go_wait"):
+                    pl.semaphore_wait(go, 1)
+                with jax.named_scope("take_low"):
+                    for j in (3, 2, 1, 0):
+                        take(low + j)
+
             @pl.when(a == 1)
             def _():
                 loop(0, NL, lambda t: attend(0, turn(t), a, 0, LVL, False, last=True))
+
+                @pl.when(even)
+                def _():
+                    for j in (shard, NL + partner, NL + far, NL + far2, b, partner):
+                        for what in ("k", "v"):
+                            hop(j, what, 2).wait_send()
+                    pl.semaphore_signal(go, inc=1, device_id=(d, a, partner), device_id_type=MESH)
 
             @pl.when(a > 1)
             def _():
@@ -367,11 +380,23 @@
 
         @pl.when(host)
         def _():
+            with jax.named_scope("host_wait"):
+                for j in range(NL):
+                    wait_piece(3 * NL + j)
+                for j in range(NL):
+                    wait_q(1, j)
+            own_block(1)
+            with jax.named_scope("host_att"):
+                loop(0, NL, lambda i: attend(1, i, 3, 2 * LVL, LVL, False))
+                loop(0, NL, lambda i: attend(1, i, 3, LVL, LVL, True))
             with jax.named_scope("take2"):
                 for j in (b, partner, far, far2):
                     take(j)
             with jax.named_scope("att2"):
                 loop(0, NL, lambda t: attend(0, turn(t), a, 0, LVL, True, last=True))
+            with jax.named_scope("host_last"):
+                finish(1, NL - 1)
+                loop(0, NL - 1, lambda i: attend(1, i, 3, 256, 512, True, last=True))
 
         @pl.when((a >= 2) & (odd == 1))
         def _():
@@ -410,25 +435,6 @@
             with jax.named_scope("att3b"):
                 attend(0, 0, a, 256, 128, True, last=True)
 
-    @pl.when(host)
-    def _():
-        with jax.named_scope("host_wait"):
-            for j in range(NL):
-                wait_piece(3 * NL + j)
-            for j in range(NL):
-                wait_q(1, j)
-        own_block(1)
-
-        def each(i):
-            attend(1, i, 3, 2 * LVL, LVL, False)
-
-            @pl.when(i < NL - 1)
-            def _():
-                attend(1, i, 3, 256, 512, True)
-            attend(1, i, 3, LVL, LVL, True, last=True)
-        with jax.named_scope("host_att"):
-            loop(0, NL, each)
-
     def take_o(h):
         @pl.when((b != h) | ((a == 3) & (h % 2 == 0)))
         def _():
@@ -446,14 +452,20 @@
     for cols in tiles:
         y_acc[:, cols] = project_o(0, cols) + project_o(2, cols)
     with jax.named_scope("o_odd"):
-        take_o(1)
-        take_o(3)
-    y_copies = []
-    with jax.named_scope("y_out"):
-        for t, cols in enumerate(tiles):
-            y_tile[:, cols] = (y_acc[:, cols] + project_o(1, cols) + project_o(3, cols)).astype(BF)
-            y_copies.append(pltpu.make_async_copy(y_tile.at[:, cols], y_ref.at[:, cols], ysem.at[t]))
-            y_copies[-1].start()
+        for h in (1, 3):
+            @pl.when(b // 2 == h // 2)
+            def _():
+                take_o(h)
+                for cols in tiles:
+                    y_acc[:, cols] += project_o(h, cols)
+        for h in (1, 3):
+            @pl.when(b // 2 != h // 2)
+            def _():
+                take_o(h)
+                for t, cols in enumerate(tiles):
+                    y_tile[:, cols] = (y_acc[:, cols] + project_o(h, cols)).astype(BF)
+                    pltpu.make_async_copy(y_tile.at[:, cols], y_ref.at[:, cols], ysem.at[t]).start()
+    y_copies = [pltpu.make_async_copy(y_tile.at[:, cols], y_ref.at[:, cols], ysem.at[t]) for t, cols in enumerate(tiles)]
 
     for h in range(NL):
         @pl.when(b != h)
@@ -506,8 +518,8 @@
                 pltpu.VMEM((NL, TOK, HD), BF), pltpu.VMEM((NL, TOK, HD), BF), pltpu.VMEM((NL, 2, TOK, HD), BF),
                 pltpu.VMEM((16 * TOK, HD), BF), pltpu.VMEM((16 * TOK, HD), BF),
                 pltpu.VMEM((2, NL, 2, TOK, HD), BF), pltpu.VMEM((TOK, 2 * NL * HD), BF),
-                pltpu.VMEM((2, NL, TOK, 2 * HD), BF), pltpu.VMEM((NL, 2, TOK, HD), F32),
-                pltpu.VMEM((NL, 2, TOK, LANES), F32), pltpu.VMEM((NL, 2, TOK, LANES), F32),
+                pltpu.VMEM((2, NL, TOK, 2 * HD), BF), pltpu.VMEM((2, NL, 2, TOK, HD), F32),
+                pltpu.VMEM((2, NL, 2, TOK, LANES), F32), pltpu.VMEM((2, NL, 2, TOK, LANES), F32),
                 pltpu.VMEM((TOK, DM), F32), pltpu.VMEM((TOK, DM), BF),
                 dma((2,)), dma(()), dma((KCUT,)), dma((KCUT,)), dma((QCUT,)), dma(()),
                 dma((16,)), dma((16,)), dma((16,)), dma((16,)), dma((NL,)),

time: 64.9 us -> 58.8 us (0.906)
  the two profiles are of different devices: /device:TPU:26 before, /device:TPU:30 now
where the time goes in v5:
time: 58.8 us; the launch traced here: 58.6 us
  Pallas kernels  56.4 us (96%)
  local copies, waits for them, and re-layouts  2.21 us (4%)
    pallas_call x1, Pallas kernels, local_fn(): pl.pallas_call(body, out_shape=jax.ShapeDtypeStruct((TOK, DM), BF), in_sp...  56.4 us
    unnamed x1, local copies, waits for them, and re-layouts  2.21 us

profile of v5, /device:TPU:30, one launch (start us, length us, event | category | flops | bytes accessed | tf_op | source)
XLA Modules:
  0.0 58.6 jit_solution(4002274824503598942)
XLA Ops:
  0.0 56.4 %shard_map.73 = bf16[192,2560]{1,0:T(8,128)(2,1)} custom-call(f32[2,192,128]{2,1,0:T(8,128)} %constant.4.clone.trig_hbm, f32[2,16,128]{2,1,0:T(8,128)} %constant.5.clone.base_hbm, bf16[192,2560]{1,0:T(8,128)(2,1)} %x_hbm.1, bf16[2560,8,256]{2,1,0:T(8,128)(2,1)} %wq_hbm.1, bf16[2560,4,256]{2,1,0:T(4,128)(2,1)} %wk_hbm.1, bf16[2560,4,256]{2,1,0:T(4,128)(2,1)} %wv_hbm.1, ...), custom_call_target="tpu_custom_call" | custom-call | tf_op jit(solution)/shard_map/pallas_call | solution.py:509
  56.4 2.2 %copy.9 = bf16[192,2560]{1,0:T(8,128)(2,1)} copy(bf16[192,2560]{1,0:T(8,128)(2,1)} %shard_map.73) | data formatting | bytes 1966080

commit v6 on v5

--- a/solution.py
+++ b/solution.py
@@ -26,9 +26,9 @@
 
 
 def body(trig_hbm, base_hbm, x_hbm, wq_hbm, wk_hbm, wv_hbm, wo_hbm, y_ref,
-         trig, base, x, wq, wk, wv, wo, ko, vo, qo, kb, vb, qb, ob, osend, acc, m_s, l_s, y_acc, y_tile,
+         trig, base, x, wq, wk, wv, wo, ko, vo, qo, kb, vb, qb, ob, osend, acc, m_s, l_s, y_acc,
          tsem, xsem, wksem, wvsem, wqsem, wosem, krecv, vrecv, kfs, vfs, qfs, ksend, vsend, qsend, qrecv,
-         os_sem, orecv, ysem, go):
+         os_sem, orecv, go):
     d, a, b = lax.axis_index("dp"), lax.axis_index("cpo"), lax.axis_index("cpi")
     shard = a * NL + b
     odd = lax.rem(b, 2)
@@ -48,8 +48,7 @@
 
     xcopy = pltpu.make_async_copy(x_hbm, x, xsem)
     xcopy.start()
-    for c in range(KCUT):
-        cut(wk_hbm, wk, wksem, KCUT, c).start()
+    cut(wk_hbm, wk, wksem, KCUT, 0).start()
     trig_copy = pltpu.make_async_copy(trig_hbm, trig, tsem.at[0])
     base_copy = pltpu.make_async_copy(base_hbm, base, tsem.at[1])
 
@@ -118,11 +117,17 @@
             return remote(vo.at[h], vb.at[rows(shard)], vsend.at[h], vrecv.at[shard], dev)
         return remote(qo.at[h], qb.at[0, b], qsend.at[h], qrecv.at[0, b], dev)
 
-    def send(what, heads):
-        for h in heads:
-            @pl.when(b != h)
-            def _():
-                exchange(h, what).start()
+    def send(what, early=True, late=True):
+        for h in (0, 2, 1, 3):
+            soon = (partner == h) | (h % 2 == 0)
+            if early:
+                @pl.when((b != h) & soon)
+                def _():
+                    exchange(h, what).start()
+            if late:
+                @pl.when((b != h) & jnp.logical_not(soon))
+                def _():
+                    exchange(h, what).start()
 
     def hop(s, what, level):
         dev = (d, level, b)
@@ -157,6 +162,8 @@
     first_user = even | (a >= 1)
 
     xcopy.wait()
+    for c in range(1, KCUT):
+        cut(wk_hbm, wk, wksem, KCUT, c).start()
 
     def start_v():
         trig_copy.start()
@@ -182,7 +189,7 @@
     with jax.named_scope("barrier"):
         pl.semaphore_wait(bar, 3 + one(a > 0) + one(a < NL - 1) + 3 * one(host) + one(a == 3)
                           + one((a == 3) & (odd == 1)))
-    send("k", (0, 2))
+    send("k", late=False)
 
     def relay(who, whats, js):
         @pl.when(who)
@@ -198,13 +205,13 @@
 
     with jax.named_scope("v_proj"):
         v_f = project(wv, KCUT, [cut(wv_hbm, wv, wvsem, KCUT, c) for c in range(KCUT)], NL, {1: start_q},
-                      {2: lambda: relay(even, ("k",), (partner,))})
+                      {2: lambda: relay(even | (a >= 1), ("k",), (partner,))})
     for h in range(NL):
         vo[h] = v_f[:, h * HD:(h + 1) * HD].astype(BF)
     vb[rows(shard), :] = vo[b]
-    send("v", (0, 2))
-    send("k", (1, 3))
-    send("v", (1, 3))
+    send("v", late=False)
+    send("k", early=False)
+    send("v", early=False)
 
     @pl.when(first_user)
     def _():
@@ -213,7 +220,7 @@
     def relay_1():
         relay(even, ("v",), (partner,))
         relay(even, ("k",), (far, far2))
-        relay((odd == 1) & (a >= 1), ("k", "v"), (partner,))
+        relay((odd == 1) & (a >= 1), ("v",), (partner,))
 
     with jax.named_scope("q_proj"):
         q_f = project(wq, QCUT, [cut(wq_hbm, wq, wqsem, QCUT, c) for c in range(QCUT)], 2 * NL,
@@ -221,7 +228,7 @@
     for h in range(2 * NL):
         qo[h // 2, h % 2, :, :HALF], qo[h // 2, h % 2, :, HALF:] = rotate(q_f, h, cos, sin)
     qb[0, b] = qo[b]
-    send("q", (0, 2, 1, 3))
+    send("q")
 
     def wide(t, n):
         return jnp.concatenate([t] * (n // LANES), axis=1)
@@ -326,10 +333,14 @@
                 take(low + j)
 
     with jax.named_scope("own_q"):
-        for j in (partner, far, far2):
-            @pl.when(jnp.logical_not(donor))
-            def _():
-                wait_q(0, j)
+        @pl.when(jnp.logical_not(donor))
+        def _():
+            wait_q(0, partner)
+
+        @pl.when(jnp.logical_not(donor | host))
+        def _():
+            wait_q(0, far)
+            wait_q(0, far2)
 
     @pl.when(donor)
     def _():
@@ -338,7 +349,50 @@
             wait_q(0, j)
             q_down(j).start()
 
-    @pl.when(jnp.logical_not(donor))
+    def chip_block(slot, here):
+        for i in range(0, NL, 2):
+            @pl.when((near0 == i) == here)
+            def _():
+                for j in (i, i + 1):
+                    attend(slot, j, a + slot, (a + slot) * LVL, OWN_KEYS[j], True, first=True)
+
+    def pair(start, fn):
+        loop(0, 2, lambda t: fn(start + t))
+
+    @pl.when(host)
+    def _():
+        with jax.named_scope("take1"):
+            for j in (b, partner, far, far2):
+                take(low + j)
+        for here in (True, False):
+            first = near0 if here else away0
+            with jax.named_scope("hq0"):
+                if not here:
+                    wait_q(0, far)
+                    wait_q(0, far2)
+            with jax.named_scope("job0"):
+                chip_block(0, here)
+                pair(first, lambda i: attend(0, i, a, (a - 1) * LVL, LVL, False))
+            with jax.named_scope("hq1"):
+                if here:
+                    for j in range(NL):
+                        wait_piece(3 * NL + j)
+                for j in ((b, partner) if here else (far, far2)):
+                    wait_q(1, j)
+            with jax.named_scope("job1"):
+                chip_block(1, here)
+                pair(first, lambda i: attend(1, i, 3, 2 * LVL, LVL, False))
+                pair(first, lambda i: attend(1, i, 3, LVL, LVL, True))
+        with jax.named_scope("take2"):
+            for j in (b, partner, far, far2):
+                take(j)
+        with jax.named_scope("host_last"):
+            finish(1, NL - 1)
+            loop(0, NL - 1, lambda i: attend(1, i, 3, 256, 512, True, last=True))
+        with jax.named_scope("att2"):
+            loop(0, NL, lambda t: attend(0, turn(t), a, 0, LVL, True, last=True))
+
+    @pl.when(jnp.logical_not(donor | host))
     def _():
         own_block(0)
 
@@ -348,12 +402,6 @@
 
         @pl.when(a > 0)
         def _():
-            @pl.when(host)
-            def _():
-                with jax.named_scope("take1"):
-                    for j in (b, partner, far, far2):
-                        take(low + j)
-
             @pl.when((a == 1) & (odd == 1))
             def _():
                 with jax.named_scope("go_wait"):
@@ -377,26 +425,6 @@
             def _():
                 with jax.named_scope("att1"):
                     loop(0, NL, lambda i: attend(0, i, a, (a - 1) * LVL, LVL, False))
-
-        @pl.when(host)
-        def _():
-            with jax.named_scope("host_wait"):
-                for j in range(NL):
-                    wait_piece(3 * NL + j)
-                for j in range(NL):
-                    wait_q(1, j)
-            own_block(1)
-            with jax.named_scope("host_att"):
-                loop(0, NL, lambda i: attend(1, i, 3, 2 * LVL, LVL, False))
-                loop(0, NL, lambda i: attend(1, i, 3, LVL, LVL, True))
-            with jax.named_scope("take2"):
-                for j in (b, partner, far, far2):
-                    take(j)
-            with jax.named_scope("att2"):
-                loop(0, NL, lambda t: attend(0, turn(t), a, 0, LVL, True, last=True))
-            with jax.named_scope("host_last"):
-                finish(1, NL - 1)
-                loop(0, NL - 1, lambda i: attend(1, i, 3, 256, 512, True, last=True))
 
         @pl.when((a >= 2) & (odd == 1))
         def _():
@@ -462,10 +490,8 @@
             @pl.when(b // 2 != h // 2)
             def _():
                 take_o(h)
-                for t, cols in enumerate(tiles):
-                    y_tile[:, cols] = (y_acc[:, cols] + project_o(h, cols)).astype(BF)
-                    pltpu.make_async_copy(y_tile.at[:, cols], y_ref.at[:, cols], ysem.at[t]).start()
-    y_copies = [pltpu.make_async_copy(y_tile.at[:, cols], y_ref.at[:, cols], ysem.at[t]) for t, cols in enumerate(tiles)]
+                for cols in tiles:
+                    y_ref[:, cols] = (y_acc[:, cols] + project_o(h, cols)).astype(BF)
 
     for h in range(NL):
         @pl.when(b != h)
@@ -494,8 +520,6 @@
         def _():
             for what in ("k", "v"):
                 hop(s, what, a + 1).wait_send()
-    for c in y_copies:
-        c.wait()
 
 
 def solution(mesh):
@@ -510,7 +534,7 @@
             body,
             out_shape=jax.ShapeDtypeStruct((TOK, DM), BF),
             in_specs=[hbm] * 7,
-            out_specs=hbm,
+            out_specs=pl.BlockSpec(memory_space=pltpu.VMEM),
             scratch_shapes=[
                 pltpu.VMEM((2, TOK, HALF), F32), pltpu.VMEM((2, NL * NL, HALF), F32),
                 pltpu.VMEM((TOK, DM), BF), pltpu.VMEM((DM, 2 * NL, HD), BF), pltpu.VMEM((DM, NL, HD), BF),
@@ -520,10 +544,10 @@
                 pltpu.VMEM((2, NL, 2, TOK, HD), BF), pltpu.VMEM((TOK, 2 * NL * HD), BF),
                 pltpu.VMEM((2, NL, TOK, 2 * HD), BF), pltpu.VMEM((2, NL, 2, TOK, HD), F32),
                 pltpu.VMEM((2, NL, 2, TOK, LANES), F32), pltpu.VMEM((2, NL, 2, TOK, LANES), F32),
-                pltpu.VMEM((TOK, DM), F32), pltpu.VMEM((TOK, DM), BF),
+                pltpu.VMEM((TOK, DM), F32),
                 dma((2,)), dma(()), dma((KCUT,)), dma((KCUT,)), dma((QCUT,)), dma(()),
                 dma((16,)), dma((16,)), dma((16,)), dma((16,)), dma((NL,)),
-                dma((NL,)), dma((NL,)), dma((NL,)), dma((2, NL)), dma((2, NL)), dma((NL,)), dma((DM // YCOLS,)),
+                dma((NL,)), dma((NL,)), dma((NL,)), dma((2, NL)), dma((2, NL)), dma((NL,)),
                 pltpu.SemaphoreType.REGULAR,
             ],
             compiler_params=pltpu.CompilerParams(collective_id=0, has_side_effects=True,

time: 58.8 us -> 58.2 us (0.990)
  the two profiles are of different devices: /device:TPU:30 before, /device:TPU:17 now
where the time goes in v6:
time: 58.2 us; the launch traced here: 58 us
  Pallas kernels  55.8 us (96%)
  local copies, waits for them, and re-layouts  2.21 us (4%)
    pallas_call x1, Pallas kernels, local_fn(): pl.pallas_call(body, out_shape=jax.ShapeDtypeStruct((TOK, DM), BF), in_sp...  55.8 us
    unnamed x1, local copies, waits for them, and re-layouts  2.21 us

profile of v6, /device:TPU:17, one launch (start us, length us, event | category | flops | bytes accessed | tf_op | source)
XLA Modules:
  0.0 58.0 jit_solution(15867434687116536762)
XLA Ops:
  0.0 55.8 %shard_map.73 = bf16[192,2560]{1,0:T(8,128)(2,1)} custom-call(f32[2,192,128]{2,1,0:T(8,128)} %constant.4.clone.trig_hbm, f32[2,16,128]{2,1,0:T(8,128)} %constant.5.clone.base_hbm, bf16[192,2560]{1,0:T(8,128)(2,1)} %x_hbm.1, bf16[2560,8,256]{2,1,0:T(8,128)(2,1)} %wq_hbm.1, bf16[2560,4,256]{2,1,0:T(4,128)(2,1)} %wk_hbm.1, bf16[2560,4,256]{2,1,0:T(4,128)(2,1)} %wv_hbm.1, ...), custom_call_target="tpu_custom_call" | custom-call | tf_op jit(solution)/shard_map/pallas_call | solution.py:533
  55.8 2.2 %copy.9 = bf16[192,2560]{1,0:T(8,128)(2,1)} copy(bf16[192,2560]{1,0:T(8,128)(2,1)} %shard_map.73) | data formatting | bytes 1966080

commit v7 on v6

--- a/solution.py
+++ b/solution.py
@@ -16,7 +16,6 @@
 HD = 256
 HALF = HD // 2
 LANES = 128
-YCOLS = 512
 NEG = -1e30
 SCALE = HD ** -0.5 * 1.4426950408889634
 KCUT = 4
@@ -26,7 +25,7 @@
 
 
 def body(trig_hbm, base_hbm, x_hbm, wq_hbm, wk_hbm, wv_hbm, wo_hbm, y_ref,
-         trig, base, x, wq, wk, wv, wo, ko, vo, qo, kb, vb, qb, ob, osend, acc, m_s, l_s, y_acc,
+         trig, base, x, wq, wk, wv, wo, ko, vo, qo, kb, vb, qb, ob, osend, acc, m_s, l_s,
          tsem, xsem, wksem, wvsem, wqsem, wosem, krecv, vrecv, kfs, vfs, qfs, ksend, vsend, qsend, qrecv,
          os_sem, orecv, go):
     d, a, b = lax.axis_index("dp"), lax.axis_index("cpo"), lax.axis_index("cpi")
@@ -91,7 +90,8 @@
             if c in fetch:
                 fetch[c]()
             r = DM // n
-            part = jnp.dot(x[:, c * r:(c + 1) * r], w[pl.ds(c * r, r)].reshape(r, heads * HD),
+            at = c * r % w.shape[0]
+            part = jnp.dot(x[:, c * r:(c + 1) * r], w[pl.ds(at, r)].reshape(r, heads * HD),
                            preferred_element_type=F32)
             total = part if total is None else total + part
             if c in between:
@@ -171,9 +171,13 @@
         for c in range(KCUT):
             cut(wv_hbm, wv, wvsem, KCUT, c).start()
 
+    def cut_q(c):
+        r = DM // QCUT
+        return pltpu.make_async_copy(wq_hbm.at[pl.ds(c * r, r)], wq.at[pl.ds(c % 2 * r, r)], wqsem.at[c])
+
     def start_q():
-        for c in range(QCUT):
-            cut(wq_hbm, wq, wqsem, QCUT, c).start()
+        cut_q(0).start()
+        cut_q(1).start()
 
     with jax.named_scope("k_proj"):
         k_f = project(wk, KCUT, [cut(wk_hbm, wk, wksem, KCUT, c) for c in range(KCUT)], NL, {1: start_v}, {})
@@ -218,13 +222,14 @@
         pass_on(shard, ("v",))
 
     def relay_1():
+        cut_q(3).start()
         relay(even, ("v",), (partner,))
         relay(even, ("k",), (far, far2))
         relay((odd == 1) & (a >= 1), ("v",), (partner,))
 
     with jax.named_scope("q_proj"):
-        q_f = project(wq, QCUT, [cut(wq_hbm, wq, wqsem, QCUT, c) for c in range(QCUT)], 2 * NL,
-                      {1: wo_copy.start}, {1: relay_1})
+        q_f = project(wq, QCUT, [cut_q(c) for c in range(QCUT)], 2 * NL,
+                      {3: wo_copy.start}, {0: cut_q(2).start, 1: relay_1})
     for h in range(2 * NL):
         qo[h // 2, h % 2, :, :HALF], qo[h // 2, h % 2, :, HALF:] = rotate(q_f, h, cos, sin)
     qb[0, b] = qo[b]
@@ -361,36 +366,56 @@
 
     @pl.when(host)
     def _():
+        def low_0(start):
+            pair(start, lambda i: attend(0, i, a, (a - 1) * LVL, LVL, False))
+
+        def low_1(start):
+            pair(start, lambda i: attend(1, i, 3, LVL, LVL, True))
+
+        def top_1(here, start):
+            with jax.named_scope("hq1"):
+                for j in ((b, partner) if here else (far, far2)):
+                    wait_q(1, j)
+            with jax.named_scope("top_1"):
+                chip_block(1, here)
+                pair(start, lambda i: attend(1, i, 3, 2 * LVL, LVL, False))
+
+        with jax.named_scope("job0"):
+            chip_block(0, True)
         with jax.named_scope("take1"):
             for j in (b, partner, far, far2):
                 take(low + j)
-        for here in (True, False):
-            first = near0 if here else away0
-            with jax.named_scope("hq0"):
-                if not here:
-                    wait_q(0, far)
-                    wait_q(0, far2)
-            with jax.named_scope("job0"):
-                chip_block(0, here)
-                pair(first, lambda i: attend(0, i, a, (a - 1) * LVL, LVL, False))
-            with jax.named_scope("hq1"):
-                if here:
-                    for j in range(NL):
-                        wait_piece(3 * NL + j)
-                for j in ((b, partner) if here else (far, far2)):
-                    wait_q(1, j)
-            with jax.named_scope("job1"):
-                chip_block(1, here)
-                pair(first, lambda i: attend(1, i, 3, 2 * LVL, LVL, False))
-                pair(first, lambda i: attend(1, i, 3, LVL, LVL, True))
+        low_0(near0)
+        with jax.named_scope("hq0"):
+            wait_q(0, far)
+            wait_q(0, far2)
+        with jax.named_scope("job0"):
+            chip_block(0, False)
+            low_0(away0)
+        with jax.named_scope("hkv1"):
+            for j in range(NL):
+                wait_piece(3 * NL + j)
+        top_1(True, near0)
+        low_1(near0)
+
+        @pl.when(near0 == 2)
+        def _():
+            finish(1, NL - 1)
+
+        top_1(False, away0)
+        low_1(away0)
+
+        @pl.when(near0 == 0)
+        def _():
+            finish(1, NL - 1)
+
         with jax.named_scope("take2"):
             for j in (b, partner, far, far2):
                 take(j)
-        with jax.named_scope("host_last"):
-            finish(1, NL - 1)
-            loop(0, NL - 1, lambda i: attend(1, i, 3, 256, 512, True, last=True))
         with jax.named_scope("att2"):
             loop(0, NL, lambda t: attend(0, turn(t), a, 0, LVL, True, last=True))
+        with jax.named_scope("host_last"):
+            loop(0, NL - 1, lambda i: attend(1, i, 3, 256, 512, True, last=True))
 
     @pl.when(jnp.logical_not(donor | host))
     def _():
@@ -472,26 +497,26 @@
         return jnp.dot(ob[:, h * 2 * HD:(h + 1) * 2 * HD], wo[pl.ds(h * 2 * HD, 2 * HD), cols],
                        preferred_element_type=F32)
 
-    tiles = [pl.ds(t * YCOLS, YCOLS) for t in range(DM // YCOLS)]
+    tiles = [(pl.ds(t * HD, HD), (t // (2 * NL), t // 2 % NL, t % 2)) for t in range(DM // HD)]
     with jax.named_scope("o_even"):
         take_o(0)
         take_o(2)
     wo_copy.wait()
-    for cols in tiles:
-        y_acc[:, cols] = project_o(0, cols) + project_o(2, cols)
+    for cols, at in tiles:
+        acc[at] = project_o(0, cols) + project_o(2, cols)
     with jax.named_scope("o_odd"):
         for h in (1, 3):
             @pl.when(b // 2 == h // 2)
             def _():
                 take_o(h)
-                for cols in tiles:
-                    y_acc[:, cols] += project_o(h, cols)
+                for cols, at in tiles:
+                    acc[at] += project_o(h, cols)
         for h in (1, 3):
             @pl.when(b // 2 != h // 2)
             def _():
                 take_o(h)
-                for cols in tiles:
-                    y_ref[:, cols] = (y_acc[:, cols] + project_o(h, cols)).astype(BF)
+                for cols, at in tiles:
+                    y_ref[:, cols] = (acc[at] + project_o(h, cols)).astype(BF)
 
     for h in range(NL):
         @pl.when(b != h)
@@ -528,7 +553,7 @@
         steps, starts = np.arange(TOK)[:, None] * freq, (np.arange(NL * NL) * TOK)[:, None] * freq
         trig = jnp.asarray(np.stack([np.cos(steps), np.sin(steps)]), F32)
         base = jnp.asarray(np.stack([np.cos(starts), np.sin(starts)]), F32)
-        hbm = pl.BlockSpec(memory_space=pl.ANY)
+        hbm = pl.BlockSpec(memory_space=pltpu.HBM)
         dma = pltpu.SemaphoreType.DMA
         return pl.pallas_call(
             body,
@@ -537,21 +562,20 @@
             out_specs=pl.BlockSpec(memory_space=pltpu.VMEM),
             scratch_shapes=[
                 pltpu.VMEM((2, TOK, HALF), F32), pltpu.VMEM((2, NL * NL, HALF), F32),
-                pltpu.VMEM((TOK, DM), BF), pltpu.VMEM((DM, 2 * NL, HD), BF), pltpu.VMEM((DM, NL, HD), BF),
+                pltpu.VMEM((TOK, DM), BF), pltpu.VMEM((DM // 2, 2 * NL, HD), BF), pltpu.VMEM((DM, NL, HD), BF),
                 pltpu.VMEM((DM, NL, HD), BF), pltpu.VMEM((2 * NL * HD, DM), BF),
                 pltpu.VMEM((NL, TOK, HD), BF), pltpu.VMEM((NL, TOK, HD), BF), pltpu.VMEM((NL, 2, TOK, HD), BF),
                 pltpu.VMEM((16 * TOK, HD), BF), pltpu.VMEM((16 * TOK, HD), BF),
                 pltpu.VMEM((2, NL, 2, TOK, HD), BF), pltpu.VMEM((TOK, 2 * NL * HD), BF),
                 pltpu.VMEM((2, NL, TOK, 2 * HD), BF), pltpu.VMEM((2, NL, 2, TOK, HD), F32),
                 pltpu.VMEM((2, NL, 2, TOK, LANES), F32), pltpu.VMEM((2, NL, 2, TOK, LANES), F32),
-                pltpu.VMEM((TOK, DM), F32),
                 dma((2,)), dma(()), dma((KCUT,)), dma((KCUT,)), dma((QCUT,)), dma(()),
                 dma((16,)), dma((16,)), dma((16,)), dma((16,)), dma((NL,)),
                 dma((NL,)), dma((NL,)), dma((NL,)), dma((2, NL)), dma((2, NL)), dma((NL,)),
                 pltpu.SemaphoreType.REGULAR,
             ],
             compiler_params=pltpu.CompilerParams(collective_id=0, has_side_effects=True,
-                                                 vmem_limit_bytes=63 * 2 ** 20),
+                                                 vmem_limit_bytes=51 * 2 ** 20),
         )(trig, base, hidden, w_q, w_k, w_v, w_o.reshape(2 * NL * HD, DM))
 
     return jax.shard_map(local_fn, mesh=mesh,

time: 58.2 us -> 56.8 us (0.976)
  the two profiles are of different devices: /device:TPU:17 before, /device:TPU:26 now
where the time goes in v7:
time: 56.8 us; the launch traced here: 56.4 us
  Pallas kernels  52.6 us (93%)
  local copies, waits for them, and re-layouts  3.79 us (7%)
    pallas_call x1, Pallas kernels, local_fn(): pl.pallas_call(body, out_shape=jax.ShapeDtypeStruct((TOK, DM), BF), in_sp...  52.6 us
    unnamed x7, local copies, waits for them, and re-layouts  3.79 us

profile of v7, /device:TPU:26, one launch (start us, length us, event | category | flops | bytes accessed | tf_op | source)
XLA Modules:
  0.0 56.4 jit_solution(1331787792142911285)
XLA Ops:
  0.0 0.0 copy-start
  0.0 1.2 %copy-done = bf16[192,2560]{1,0:T(8,128)(2,1)S(1)} copy-done((bf16[192,2560]{1,0:T(8,128)(2,1)S(1)}, bf16[192,2560]{1,0:T(8,128)(2,1)}, u32[]{:S(2)}) %copy-start) | copy-done | bytes 983064
  1.2 0.0 copy-start.1
  1.2 0.9 %copy-done.1 = f32[2,192,128]{2,1,0:T(8,128)S(1)} copy-done((f32[2,192,128]{2,1,0:T(8,128)S(1)}, f32[2,192,128]{2,1,0:T(8,128)}, u32[]{:S(2)}) %copy-start.1) | copy-done | bytes 196632
  2.1 0.0 copy-start.2
  2.1 0.7 %copy-done.2 = f32[2,16,128]{2,1,0:T(8,128)S(1)} copy-done((f32[2,16,128]{2,1,0:T(8,128)S(1)}, f32[2,16,128]{2,1,0:T(8,128)}, u32[]{:S(2)}) %copy-start.2) | copy-done | bytes 16408
  2.8 52.6 %shard_map.73 = bf16[192,2560]{1,0:T(8,128)(2,1)S(1)} custom-call(f32[2,192,128]{2,1,0:T(8,128)S(1)} %copy-done.1, f32[2,16,128]{2,1,0:T(8,128)S(1)} %copy-done.2, bf16[192,2560]{1,0:T(8,128)(2,1)S(1)} %copy-done, bf16[2560,8,256]{2,1,0:T(8,128)(2,1)} %wq_hbm.1, bf16[2560,4,256]{2,1,0:T(4,128)(2,1)} %wk_hbm.1, bf16[2560,4,256]{2,1,0:T(4,128)(2,1)} %wv_hbm.1, ...), custom_call_target="tpu_custom_call" | custom-call | tf_op jit(solution)/shard_map/pallas_call | solution.py:558
  55.5 0.9 %copy.9 = bf16[192,2560]{1,0:T(8,128)(2,1)} copy(bf16[192,2560]{1,0:T(8,128)(2,1)S(1)} %shard_map.73) | data formatting | bytes 1966080
Async XLA Ops:
  0.0 1.2 %copy-start = (bf16[192,2560]{1,0:T(8,128)(2,1)S(1)}, bf16[192,2560]{1,0:T(8,128)(2,1)}, u32[]{:S(2)}) copy-start(bf16[192,2560]{1,0:T(8,128)(2,1)} %x_hbm.1) | copy-start | bytes 2949124
  1.2 0.9 %copy-start.1 = (f32[2,192,128]{2,1,0:T(8,128)S(1)}, f32[2,192,128]{2,1,0:T(8,128)}, u32[]{:S(2)}) copy-start(f32[2,192,128]{2,1,0:T(8,128)} %constant.4.clone.trig_hbm) | copy-start | bytes 589828
  2.1 0.7 %copy-start.2 = (f32[2,16,128]{2,1,0:T(8,128)S(1)}, f32[2,16,128]{2,1,0:T(8,128)}, u32[]{:S(2)}) copy-start(f32[2,16,128]{2,1,0:T(8,128)} %constant.5.clone.base_hbm) | copy-start | bytes 49156

commit v8 on v7

--- a/solution.py
+++ b/solution.py
@@ -1,6 +1,5 @@
 import jax
 import jax.numpy as jnp
-import numpy as np
 from jax import lax
 from jax.experimental import pallas as pl
 from jax.experimental.pallas import tpu as pltpu
@@ -16,6 +15,7 @@
 HD = 256
 HALF = HD // 2
 LANES = 128
+FINE = 16
 NEG = -1e30
 SCALE = HD ** -0.5 * 1.4426950408889634
 KCUT = 4
@@ -24,9 +24,9 @@
 F32, BF = jnp.float32, jnp.bfloat16
 
 
-def body(trig_hbm, base_hbm, x_hbm, wq_hbm, wk_hbm, wv_hbm, wo_hbm, y_ref,
-         trig, base, x, wq, wk, wv, wo, ko, vo, qo, kb, vb, qb, ob, osend, acc, m_s, l_s,
-         tsem, xsem, wksem, wvsem, wqsem, wosem, krecv, vrecv, kfs, vfs, qfs, ksend, vsend, qsend, qrecv,
+def body(freq_ref, x, wq_hbm, wk_hbm, wv_hbm, wo_hbm, y_ref,
+         wq, wk, wv, wo, ko, vo, qo, kb, vb, qb, ob, osend, acc, m_s, l_s,
+         wksem, wvsem, wqsem, wosem, krecv, vrecv, kfs, vfs, qfs, ksend, vsend, qsend, qrecv,
          os_sem, orecv, go):
     d, a, b = lax.axis_index("dp"), lax.axis_index("cpo"), lax.axis_index("cpi")
     shard = a * NL + b
@@ -45,11 +45,8 @@
         r = DM // n
         return pltpu.make_async_copy(src.at[pl.ds(c * r, r)], dst.at[pl.ds(c * r, r)], sem.at[c])
 
-    xcopy = pltpu.make_async_copy(x_hbm, x, xsem)
-    xcopy.start()
-    cut(wk_hbm, wk, wksem, KCUT, 0).start()
-    trig_copy = pltpu.make_async_copy(trig_hbm, trig, tsem.at[0])
-    base_copy = pltpu.make_async_copy(base_hbm, base, tsem.at[1])
+    for c in range(KCUT):
+        cut(wk_hbm, wk, wksem, KCUT, c).start()
 
     bar = pltpu.get_barrier_semaphore()
 
@@ -82,6 +79,14 @@
 
     def one(p):
         return p.astype(jnp.int32)
+
+    step = lax.broadcasted_iota(jnp.int32, (FINE, HALF), 0)
+    fine = step.astype(F32) * freq_ref[...]
+    coarse = (step * FINE + shard * TOK).astype(F32) * freq_ref[...]
+    cf, sf = jnp.cos(fine)[None], jnp.sin(fine)[None]
+    cc, sc = jnp.cos(coarse)[:TOK // FINE, None], jnp.sin(coarse)[:TOK // FINE, None]
+    cos = (cc * cf - sc * sf).reshape(TOK, HALF)
+    sin = (sc * cf + cc * sf).reshape(TOK, HALF)
 
     def project(w, n, copies, heads, fetch, between):
         total = None
@@ -161,13 +166,8 @@
 
     first_user = even | (a >= 1)
 
-    xcopy.wait()
-    for c in range(1, KCUT):
-        cut(wk_hbm, wk, wksem, KCUT, c).start()
 
     def start_v():
-        trig_copy.start()
-        base_copy.start()
         for c in range(KCUT):
             cut(wv_hbm, wv, wvsem, KCUT, c).start()
 
@@ -182,11 +182,6 @@
     with jax.named_scope("k_proj"):
         k_f = project(wk, KCUT, [cut(wk_hbm, wk, wksem, KCUT, c) for c in range(KCUT)], NL, {1: start_v}, {})
     wo_copy = pltpu.make_async_copy(wo_hbm, wo, wosem)
-    trig_copy.wait()
-    base_copy.wait()
-    cb, sb = base[0, pl.ds(shard, 1), :], base[1, pl.ds(shard, 1), :]
-    cos = cb * trig[0] - sb * trig[1]
-    sin = sb * trig[0] + cb * trig[1]
     for h in range(NL):
         ko[h, :, :HALF], ko[h, :, HALF:] = rotate(k_f, h, cos, sin)
     kb[rows(shard), :] = ko[b]
@@ -549,34 +544,30 @@
 
 def solution(mesh):
     def local_fn(hidden, w_q, w_k, w_v, w_o):
-        freq = ROPE_BASE ** (-np.arange(HALF) * 2.0 / HD)
-        steps, starts = np.arange(TOK)[:, None] * freq, (np.arange(NL * NL) * TOK)[:, None] * freq
-        trig = jnp.asarray(np.stack([np.cos(steps), np.sin(steps)]), F32)
-        base = jnp.asarray(np.stack([np.cos(starts), np.sin(starts)]), F32)
+        freq = (ROPE_BASE ** (-jnp.arange(HALF, dtype=F32) * 2.0 / HD)).reshape(1, HALF)
         hbm = pl.BlockSpec(memory_space=pltpu.HBM)
         dma = pltpu.SemaphoreType.DMA
         return pl.pallas_call(
             body,
             out_shape=jax.ShapeDtypeStruct((TOK, DM), BF),
-            in_specs=[hbm] * 7,
+            in_specs=[pl.BlockSpec(memory_space=pltpu.VMEM)] * 2 + [hbm] * 4,
             out_specs=pl.BlockSpec(memory_space=pltpu.VMEM),
             scratch_shapes=[
-                pltpu.VMEM((2, TOK, HALF), F32), pltpu.VMEM((2, NL * NL, HALF), F32),
-                pltpu.VMEM((TOK, DM), BF), pltpu.VMEM((DM // 2, 2 * NL, HD), BF), pltpu.VMEM((DM, NL, HD), BF),
+                pltpu.VMEM((DM // 2, 2 * NL, HD), BF), pltpu.VMEM((DM, NL, HD), BF),
                 pltpu.VMEM((DM, NL, HD), BF), pltpu.VMEM((2 * NL * HD, DM), BF),
                 pltpu.VMEM((NL, TOK, HD), BF), pltpu.VMEM((NL, TOK, HD), BF), pltpu.VMEM((NL, 2, TOK, HD), BF),
                 pltpu.VMEM((16 * TOK, HD), BF), pltpu.VMEM((16 * TOK, HD), BF),
                 pltpu.VMEM((2, NL, 2, TOK, HD), BF), pltpu.VMEM((TOK, 2 * NL * HD), BF),
                 pltpu.VMEM((2, NL, TOK, 2 * HD), BF), pltpu.VMEM((2, NL, 2, TOK, HD), F32),
                 pltpu.VMEM((2, NL, 2, TOK, LANES), F32), pltpu.VMEM((2, NL, 2, TOK, LANES), F32),
-                dma((2,)), dma(()), dma((KCUT,)), dma((KCUT,)), dma((QCUT,)), dma(()),
+                dma((KCUT,)), dma((KCUT,)), dma((QCUT,)), dma(()),
                 dma((16,)), dma((16,)), dma((16,)), dma((16,)), dma((NL,)),
                 dma((NL,)), dma((NL,)), dma((NL,)), dma((2, NL)), dma((2, NL)), dma((NL,)),
                 pltpu.SemaphoreType.REGULAR,
             ],
             compiler_params=pltpu.CompilerParams(collective_id=0, has_side_effects=True,
                                                  vmem_limit_bytes=51 * 2 ** 20),
-        )(trig, base, hidden, w_q, w_k, w_v, w_o.reshape(2 * NL * HD, DM))
+        )(freq, hidden, w_q, w_k, w_v, w_o.reshape(2 * NL * HD, DM))
 
     return jax.shard_map(local_fn, mesh=mesh,
                          in_specs=(P(("dp", "cpo", "cpi"), None), P(), P(), P(), P()),

time: 56.8 us -> 54.3 us (0.956)
  local copies, waits for them, and re-layouts: 3.79 us -> 2.15 us
  Pallas kernels: 52.6 us -> 51.8 us
    unnamed x7 -> x3, local copies, waits for them, and re-layouts: 3.79 us -> 2.15 us
    pallas_call x1, Pallas kernels: 52.6 us -> 51.8 us  [local_fn(): pl.pallas_call(body, out_shape=jax.ShapeDtypeStruct((TOK, DM), BF), in_sp...]
where the time goes in v8:
time: 54.3 us; the launch traced here: 54 us
  Pallas kernels  51.8 us (95%)
  local copies, waits for them, and re-layouts  2.15 us (4%)
    pallas_call x1, Pallas kernels, local_fn(): pl.pallas_call(body, out_shape=jax.ShapeDtypeStruct((TOK, DM), BF), in_sp...  51.8 us
    unnamed x3, local copies, waits for them, and re-layouts  2.15 us

profile of v8, /device:TPU:26, one launch (start us, length us, event | category | flops | bytes accessed | tf_op | source)
XLA Modules:
  0.0 54.0 jit_solution(3535873594194159455)
XLA Ops:
  0.0 0.0 copy-start
  0.0 1.2 %copy-done = bf16[192,2560]{1,0:T(8,128)(2,1)S(1)} copy-done((bf16[192,2560]{1,0:T(8,128)(2,1)S(1)}, bf16[192,2560]{1,0:T(8,128)(2,1)}, u32[]{:S(2)}) %copy-start) | copy-done | bytes 983064
  1.2 51.8 %shard_map.55 = bf16[192,2560]{1,0:T(8,128)(2,1)S(1)} custom-call(f32[1,128]{1,0:T(1,128)S(1)} %multiply_power_fusion.freq_ref, bf16[192,2560]{1,0:T(8,128)(2,1)S(1)} %copy-done, bf16[2560,8,256]{2,1,0:T(8,128)(2,1)} %wq_hbm.1, bf16[2560,4,256]{2,1,0:T(4,128)(2,1)} %wk_hbm.1, bf16[2560,4,256]{2,1,0:T(4,128)(2,1)} %wv_hbm.1, bf16[2048,2560]{1,0:T(8,128)(2,1)} %bitcast.1), custom_call_target="tpu_custom_call" | custom-call | tf_op jit(solution)/shard_map/pallas_call | solution.py:550
  53.0 0.9 %copy.7 = bf16[192,2560]{1,0:T(8,128)(2,1)} copy(bf16[192,2560]{1,0:T(8,128)(2,1)S(1)} %shard_map.55) | data formatting | bytes 1966080
  (1 shorter events, 0.0 us)
Async XLA Ops:
  0.0 1.2 %copy-start = (bf16[192,2560]{1,0:T(8,128)(2,1)S(1)}, bf16[192,2560]{1,0:T(8,128)(2,1)}, u32[]{:S(2)}) copy-start(bf16[192,2560]{1,0:T(8,128)(2,1)} %x.1) | copy-start | bytes 2949124

commit v9 on v8

--- a/solution.py
+++ b/solution.py
@@ -332,6 +332,11 @@
             for j in (b, partner, far, far2):
                 take(low + j)
 
+    @pl.when((odd == 1) & (a == 1))
+    def _():
+        with jax.named_scope("take_early"):
+            pass
+
     with jax.named_scope("own_q"):
         @pl.when(jnp.logical_not(donor))
         def _():
@@ -407,14 +412,19 @@
         with jax.named_scope("take2"):
             for j in (b, partner, far, far2):
                 take(j)
+        with jax.named_scope("host_last"):
+            loop(0, NL - 1, lambda i: attend(1, i, 3, 256, 512, True, last=True))
         with jax.named_scope("att2"):
             loop(0, NL, lambda t: attend(0, turn(t), a, 0, LVL, True, last=True))
-        with jax.named_scope("host_last"):
-            loop(0, NL - 1, lambda i: attend(1, i, 3, 256, 512, True, last=True))
 
     @pl.when(jnp.logical_not(donor | host))
     def _():
         own_block(0)
+
+        @pl.when((a == 2) & (odd == 1))
+        def _():
+            with jax.named_scope("take_early"):
+                pass
 
         @pl.when(a == 0)
         def _():
@@ -493,39 +503,32 @@
                        preferred_element_type=F32)
 
     tiles = [(pl.ds(t * HD, HD), (t // (2 * NL), t // 2 % NL, t % 2)) for t in range(DM // HD)]
-    with jax.named_scope("o_even"):
-        take_o(0)
-        take_o(2)
     wo_copy.wait()
-    for cols, at in tiles:
-        acc[at] = project_o(0, cols) + project_o(2, cols)
-    with jax.named_scope("o_odd"):
+
+    def add_head(h, here, start=False, last=False):
+        @pl.when((b // 2 == h // 2) == here)
+        def _():
+            take_o(h)
+            for cols, at in tiles:
+                part = project_o(h, cols)
+                if not start:
+                    part = part + acc[at]
+                if last:
+                    y_ref[:, cols] = part.astype(BF)
+                else:
+                    acc[at] = part
+
+    with jax.named_scope("o_near"):
         for h in (1, 3):
-            @pl.when(b // 2 == h // 2)
-            def _():
-                take_o(h)
-                for cols, at in tiles:
-                    acc[at] += project_o(h, cols)
-        for h in (1, 3):
-            @pl.when(b // 2 != h // 2)
-            def _():
-                take_o(h)
-                for cols, at in tiles:
-                    y_ref[:, cols] = (acc[at] + project_o(h, cols)).astype(BF)
+            add_head(h, True, start=True)
+        for h in (0, 2):
+            add_head(h, True)
 
     for h in range(NL):
         @pl.when(b != h)
         def _():
             for what in ("k", "v", "q"):
                 exchange(h, what).wait_send()
-
-        @pl.when((b != h) & jnp.logical_not(donor))
-        def _():
-            back_to(0, h).wait_send()
-
-        @pl.when(host)
-        def _():
-            back_to(1, h).wait_send()
 
         @pl.when(donor)
         def _():
@@ -540,6 +543,21 @@
         def _():
             for what in ("k", "v"):
                 hop(s, what, a + 1).wait_send()
+
+    with jax.named_scope("o_far"):
+        for h in (1, 3):
+            add_head(h, False)
+        for h in (0, 2):
+            add_head(h, False, last=True)
+
+    for h in range(NL):
+        @pl.when((b != h) & jnp.logical_not(donor))
+        def _():
+            back_to(0, h).wait_send()
+
+        @pl.when(host)
+        def _():
+            back_to(1, h).wait_send()
 
 
 def solution(mesh):

time: 54.3 us -> 53.6 us (0.987)
    pallas_call x1, Pallas kernels: 51.8 us -> 51.3 us  [local_fn(): pl.pallas_call(body, out_shape=jax.ShapeDtypeStruct((TOK, DM), BF), in_sp...]
where the time goes in v9:
time: 53.6 us; the launch traced here: 53.4 us
  Pallas kernels  51.3 us (96%)
  local copies, waits for them, and re-layouts  2.15 us (4%)
    pallas_call x1, Pallas kernels, local_fn(): pl.pallas_call(body, out_shape=jax.ShapeDtypeStruct((TOK, DM), BF), in_sp...  51.3 us
    unnamed x3, local copies, waits for them, and re-layouts  2.15 us

profile of v9, /device:TPU:26, one launch (start us, length us, event | category | flops | bytes accessed | tf_op | source)
XLA Modules:
  0.0 53.4 jit_solution(9996282782865410334)
XLA Ops:
  0.0 0.0 copy-start
  0.0 1.2 %copy-done = bf16[192,2560]{1,0:T(8,128)(2,1)S(1)} copy-done((bf16[192,2560]{1,0:T(8,128)(2,1)S(1)}, bf16[192,2560]{1,0:T(8,128)(2,1)}, u32[]{:S(2)}) %copy-start) | copy-done | bytes 983064
  1.2 51.3 %shard_map.55 = bf16[192,2560]{1,0:T(8,128)(2,1)S(1)} custom-call(f32[1,128]{1,0:T(1,128)S(1)} %multiply_power_fusion.freq_ref, bf16[192,2560]{1,0:T(8,128)(2,1)S(1)} %copy-done, bf16[2560,8,256]{2,1,0:T(8,128)(2,1)} %wq_hbm.1, bf16[2560,4,256]{2,1,0:T(4,128)(2,1)} %wk_hbm.1, bf16[2560,4,256]{2,1,0:T(4,128)(2,1)} %wv_hbm.1, bf16[2048,2560]{1,0:T(8,128)(2,1)} %bitcast.1), custom_call_target="tpu_custom_call" | custom-call | tf_op jit(solution)/shard_map/pallas_call | solution.py:568
  52.5 0.9 %copy.7 = bf16[192,2560]{1,0:T(8,128)(2,1)} copy(bf16[192,2560]{1,0:T(8,128)(2,1)S(1)} %shard_map.55) | data formatting | bytes 1966080
  (1 shorter events, 0.0 us)
Async XLA Ops:
  0.0 1.2 %copy-start = (bf16[192,2560]{1,0:T(8,128)(2,1)S(1)}, bf16[192,2560]{1,0:T(8,128)(2,1)}, u32[]{:S(2)}) copy-start(bf16[192,2560]{1,0:T(8,128)(2,1)} %x.1) | copy-start | bytes 2949124

commit v10 on v9

--- a/solution.py
+++ b/solution.py
@@ -18,7 +18,7 @@
 FINE = 16
 NEG = -1e30
 SCALE = HD ** -0.5 * 1.4426950408889634
-KCUT = 4
+KCUT = 5
 QCUT = 4
 OWN_KEYS = (256, 384, 640, 768)
 F32, BF = jnp.float32, jnp.bfloat16

time: 53.6 us -> 53.7 us (level)
  no operation moved by 1% of the time
where the time goes in v10:
time: 53.7 us; the launch traced here: 53.5 us
  Pallas kernels  51.3 us (96%)
  local copies, waits for them, and re-layouts  2.15 us (4%)
    pallas_call x1, Pallas kernels, local_fn(): pl.pallas_call(body, out_shape=jax.ShapeDtypeStruct((TOK, DM), BF), in_sp...  51.3 us
    unnamed x3, local copies, waits for them, and re-layouts  2.15 us

profile of v10, /device:TPU:26, one launch (start us, length us, event | category | flops | bytes accessed | tf_op | source)
XLA Modules:
  0.0 53.5 jit_solution(4615180905025168512)
XLA Ops:
  0.0 0.0 copy-start
  0.0 1.2 %copy-done = bf16[192,2560]{1,0:T(8,128)(2,1)S(1)} copy-done((bf16[192,2560]{1,0:T(8,128)(2,1)S(1)}, bf16[192,2560]{1,0:T(8,128)(2,1)}, u32[]{:S(2)}) %copy-start) | copy-done | bytes 983064
  1.2 51.3 %shard_map.55 = bf16[192,2560]{1,0:T(8,128)(2,1)S(1)} custom-call(f32[1,128]{1,0:T(1,128)S(1)} %multiply_power_fusion.freq_ref, bf16[192,2560]{1,0:T(8,128)(2,1)S(1)} %copy-done, bf16[2560,8,256]{2,1,0:T(8,128)(2,1)} %wq_hbm.1, bf16[2560,4,256]{2,1,0:T(4,128)(2,1)} %wk_hbm.1, bf16[2560,4,256]{2,1,0:T(4,128)(2,1)} %wv_hbm.1, bf16[2048,2560]{1,0:T(8,128)(2,1)} %bitcast.1), custom_call_target="tpu_custom_call" | custom-call | tf_op jit(solution)/shard_map/pallas_call | solution.py:568
  52.6 0.9 %copy.7 = bf16[192,2560]{1,0:T(8,128)(2,1)} copy(bf16[192,2560]{1,0:T(8,128)(2,1)S(1)} %shard_map.55) | data formatting | bytes 1966080
  (1 shorter events, 0.0 us)
Async XLA Ops:
  0.0 1.2 %copy-start = (bf16[192,2560]{1,0:T(8,128)(2,1)S(1)}, bf16[192,2560]{1,0:T(8,128)(2,1)}, u32[]{:S(2)}) copy-start(bf16[192,2560]{1,0:T(8,128)(2,1)} %x.1) | copy-start | bytes 2949124
